TPU v7x, 32 devices: a whole 2x2x4 slice. The times are simulated.
32 devices in a mesh: dz: 4 (over z), dy: 2 (over y), dx: 4 (over x, core).
Axes of the slice: x: 2, y: 2, z: 4, core: 2. Of those that a mesh axis runs over, the one named last changes fastest.
Arguments:
- act_one: bfloat16 [65536, 1024], P(('dz', 'dy', 'dx'))
- pre_one: bfloat16 [65536, 4096], P(('dz', 'dy', 'dx'))
- act_two: bfloat16 [65536, 1024], P(('dz', 'dy', 'dx'))
- pre_two: bfloat16 [65536, 4096], P(('dz', 'dy', 'dx'))
- grad_out: bfloat16 [65536, 1024], P(('dz', 'dy', 'dx'))
- w_in_two: bfloat16 [1024, 4096], replicated
- w_out_one: bfloat16 [4096, 1024], replicated
- w_out_two: bfloat16 [4096, 1024], replicated
Outputs:
- output: float32 [16777216], P(('dx', 'dy', 'dz'))
All inputs are finite; a program needn't handle non-finite values.
Results may differ from a plain program's by a relative error of at most 0.00156588.
Values are sent between devices in bfloat16 or wider.
A program may use at most 1 GiB of HBM per device.

v0:
```python
import jax
import jax.numpy as jnp
from jax import lax
from jax.sharding import PartitionSpec as P, NamedSharding

N_MICRO = 2


def gelu_pair(pre):
    pre_wide = pre.astype(jnp.float32)
    hidden, pull_back = jax.vjp(jax.nn.gelu, pre_wide)
    return hidden, pull_back(jnp.ones_like(pre_wide))[0]


def local_grads(act_one, pre_one, act_two, pre_two, grad_out, w_in_two, w_out_one, w_out_two):
    hid_two, slope_two = gelu_pair(pre_two)
    hid_two = hid_two.astype(jnp.bfloat16)
    g_out_two = jnp.einsum('mtf,mtd->mfd', hid_two, grad_out, preferred_element_type=jnp.float32).astype(jnp.bfloat16)
    d_hid_two = jnp.einsum('mtd,fd->mtf', grad_out, w_out_two, preferred_element_type=jnp.float32)
    d_pre_two = (d_hid_two * slope_two).astype(jnp.bfloat16)
    g_in_two = jnp.einsum('mtd,mtf->mdf', act_two, d_pre_two, preferred_element_type=jnp.float32).astype(jnp.bfloat16)
    d_back_two = jnp.einsum('mtf,df->mtd', d_pre_two, w_in_two, preferred_element_type=jnp.float32)
    d_act_two = (grad_out.astype(jnp.float32) + d_back_two).astype(jnp.bfloat16)
    hid_one, slope_one = gelu_pair(pre_one)
    hid_one = hid_one.astype(jnp.bfloat16)
    g_out_one = jnp.einsum('mtf,mtd->mfd', hid_one, d_act_two, preferred_element_type=jnp.float32).astype(jnp.bfloat16)
    d_hid_one = jnp.einsum('mtd,fd->mtf', d_act_two, w_out_one, preferred_element_type=jnp.float32)
    d_pre_one = (d_hid_one * slope_one).astype(jnp.bfloat16)
    g_in_one = jnp.einsum('mtd,mtf->mdf', act_one, d_pre_one, preferred_element_type=jnp.float32).astype(jnp.bfloat16)
    batch_count = act_one.shape[0]
    return jnp.concatenate([grad_piece.reshape(batch_count, -1) for grad_piece in (g_out_two, g_in_two, g_out_one, g_in_one)], axis=1)


def solution(mesh):
    group_size = mesh.shape['dx']
    row_spec = P(('dz', 'dy', 'dx'), None)
    full_spec = P(None, None)

    def per_device(act_one, pre_one, act_two, pre_two, grad_out, w_in_two, w_out_one, w_out_two):
        micro_rows = act_one.shape[0] // N_MICRO
        split_rows = [array_in.reshape(N_MICRO, micro_rows, array_in.shape[1]) for array_in in (act_one, pre_one, act_two, pre_two, grad_out)]
        grad_rows = local_grads(*split_rows, w_in_two, w_out_one, w_out_two)
        total_len = grad_rows.shape[1]
        outgoing = grad_rows.reshape(N_MICRO, group_size, total_len // group_size)
        incoming = lax.all_to_all(outgoing, 'dx', 1, 1, tiled=True)
        part_sum = jnp.sum(incoming, axis=(0, 1), dtype=jnp.float32)
        part_sum = lax.psum_scatter(part_sum, 'dy', scatter_dimension=0, tiled=True)
        return lax.psum_scatter(part_sum, 'dz', scatter_dimension=0, tiled=True)

    return jax.shard_map(per_device, mesh=mesh, in_specs=(row_spec,) * 5 + (full_spec,) * 3, out_specs=P(('dx', 'dy', 'dz')), check_vma=False)
```

profile of v0, /device:TPU:0, one launch (start us, length us, event | category | flops | bytes accessed | tf_op | source)
XLA Modules:
  0.0 2119.0 jit_solution(8642409864218550594)
XLA Ops:
  6.5 0.0 all-reduce.5.cloned.1.call-start
  6.5 0.0 slice-start
  6.5 30.3 %fusion.34 = bf16[2,4096,1024]{2,1,0:T(8,128)(2,1)} fusion(bf16[2,1024,1024]{2,1,0:T(8,128)(2,1)} %bitcast.38, bf16[2,1024,4096]{2,1,0:T(8,128)(2,1)} %bitcast.32), kind=kOutput, calls=%fused_computation.45 | convolution fusion | flops 17272143872 | bytes 37748736 | tf_op jit(solution)/shard_map/mtf,mtd->mfd/dot_general | solution.py:18
  36.9 0.0 slice-start.1
  36.9 0.0 copy-start
  36.9 43.8 %fusion.9 = bf16[2,1024,4096]{2,1,0:T(8,128)(2,1)} fusion(bf16[2,1024,4096]{2,1,0:T(8,128)(2,1)} %bitcast.33, bf16[2,1024,1024]{2,1,0:T(8,128)(2,1)} %bitcast.39, bf16[4096,1024]{1,0:T(8,128)(2,1)} %param.15), kind=kOutput, calls=%fused_computation.21 | convolution fusion | flops 17347641344 | bytes 46137344 | tf_op jit(solution)/shard_map/mtd,fd->mtf/dot_general | solution.py:19
  80.7 0.0 slice-done
  80.7 0.0 slice-done.1
  80.7 0.0 copy-done
  80.7 21.7 %add_convert_fusion = bf16[2,1024,1024]{2,1,0:T(8,128)(2,1)} fusion(bf16[2,1024,1024]{2,1,0:T(8,128)(2,1)S(1)} %bitcast.40, bf16[2,1024,4096]{2,1,0:T(8,128)(2,1)} %fusion.9, bf16[1024,4096]{1,0:T(8,128)(2,1)S(1)} %bitcast.37), kind=kOutput, calls=%fused_computation.52 | convolution fusion | flops 17186160640 | bytes 33554432 | tf_op jit(solution)/shard_map/mtf,df->mtd/dot_general | solution.py:22
  102.5 0.0 copy-start.3
  102.5 25.3 %fusion.42 = f32[2,1024,4096]{2,1,0:T(8,128)} fusion(bf16[2,1024,1024]{2,1,0:T(8,128)(2,1)} %add_convert_fusion, bf16[4096,1024]{1,0:T(8,128)(2,1)} %param.14), kind=kOutput, calls=%fused_computation.47 | convolution fusion | flops 17179869184 | bytes 46137344 | tf_op jit(solution)/shard_map/mtd,fd->mtf/dot_general | solution.py:27
  127.8 0.0 copy-done.3
  127.8 29.8 %fusion.37 = bf16[2,4096,1024]{2,1,0:T(8,128)(2,1)} fusion(bf16[2,1024,1024]{2,1,0:T(8,128)(2,1)S(1)} %copy-done.3, bf16[2,1024,4096]{2,1,0:T(8,128)(2,1)} %bitcast.34), kind=kOutput, calls=%fused_computation.46 | convolution fusion | flops 17272143872 | bytes 37748736 | tf_op jit(solution)/shard_map/mtf,mtd->mfd/dot_general | solution.py:26
  157.5 41.9 %convert_bitcast_fusion = bf16[2,1024,4096]{1,2,0:T(8,128)(2,1)} fusion(bf16[2,1024,1024]{2,1,0:T(8,128)(2,1)} %bitcast.41, f32[2,1024,4096]{2,1,0:T(8,128)} %fusion.42, bf16[2,1024,4096]{2,1,0:T(8,128)(2,1)} %bitcast.35), kind=kOutput, calls=%fused_computation.34 | convolution fusion | flops 17356029952 | bytes 71303168 | tf_op jit(solution)/shard_map/mtd,mtf->mdf/dot_general | solution.py:29
  199.4 21.6 %copy.24 = bf16[2,1024,4096]{2,1,0:T(8,128)(2,1)} copy(bf16[2,1024,4096]{1,2,0:T(8,128)(2,1)} %convert_bitcast_fusion) | data formatting | bytes 33554432 | tf_op jit(solution)/shard_map/convert_element_type | solution.py:29
  221.0 26.2 %concatenate.15 = bf16[2,1,4194304]{2,0,1:T(2,128)(2,1)} reshape(bf16[2,1024,4096]{2,1,0:T(8,128)(2,1)} %copy.24) | data formatting | bytes 33554432 | tf_op jit(solution)/shard_map/concatenate | solution.py:31
  247.2 25.8 %concatenate.14 = bf16[2,1,4194304]{2,0,1:T(2,128)(2,1)} reshape(bf16[2,4096,1024]{2,1,0:T(8,128)(2,1)} %fusion.37) | data formatting | bytes 33554432 | tf_op jit(solution)/shard_map/concatenate | solution.py:31
  273.0 24.8 %convert_bitcast_fusion.1 = bf16[2,1024,4096]{1,2,0:T(8,128)(2,1)} fusion(bf16[2,1024,4096]{2,1,0:T(8,128)(2,1)} %fusion.9, bf16[2,1024,1024]{2,1,0:T(8,128)(2,1)} %bitcast.42), kind=kOutput, calls=%fused_computation.35 | convolution fusion | flops 17188257792 | bytes 37748736 | tf_op jit(solution)/shard_map/mtd,mtf->mdf/dot_general | solution.py:21
  297.8 21.3 %copy.21 = bf16[2,1024,4096]{2,1,0:T(8,128)(2,1)} copy(bf16[2,1024,4096]{1,2,0:T(8,128)(2,1)} %convert_bitcast_fusion.1) | data formatting | bytes 33554432 | tf_op jit(solution)/shard_map/convert_element_type | solution.py:21
  319.1 25.9 %concatenate.13 = bf16[2,1,4194304]{2,0,1:T(2,128)(2,1)} reshape(bf16[2,1024,4096]{2,1,0:T(8,128)(2,1)} %copy.21) | data formatting | bytes 33554432 | tf_op jit(solution)/shard_map/concatenate | solution.py:31
  345.0 25.9 %concatenate.12 = bf16[2,1,4194304]{2,0,1:T(2,128)(2,1)} reshape(bf16[2,4096,1024]{2,1,0:T(8,128)(2,1)} %fusion.34) | data formatting | bytes 33554432 | tf_op jit(solution)/shard_map/concatenate | solution.py:31
  370.9 128.4 %pad_maximum_fusion = bf16[2,4,4194304]{2,0,1:T(2,128)(2,1)} fusion(bf16[2,1,4194304]{2,0,1:T(2,128)(2,1)} %concatenate.15, bf16[2,1,4194304]{2,0,1:T(2,128)(2,1)} %concatenate.14, bf16[2,1,4194304]{2,0,1:T(2,128)(2,1)} %concatenate.13, bf16[2,1,4194304]{2,0,1:T(2,128)(2,1)} %concatenate.12), kind=kLoop, calls=%fused_computation.1 | loop fusion | flops 100663296 | bytes 134217728 | tf_op jit(solution)/shard_map/concatenate | solution.py:31
  499.3 755.1 %all_to_all.5 = bf16[2,4,4194304]{2,0,1:T(2,128)(2,1)} all-to-all(bf16[2,4,4194304]{2,0,1:T(2,128)(2,1)} %pad_maximum_fusion), channel_id=1, replica_groups=mesh['dz'=4,'dy'=2,'dx'=4] {'dx'}, dimensions={1} | all-to-all | bytes 134217728 | tf_op jit(solution)/shard_map/all_to_all | solution.py:45
  1254.4 0.0 copy-start.2
  1254.5 180.4 %convert_reduce_fusion = f32[4194304]{0:T(1024)} fusion(bf16[2,4,4194304]{2,0,1:T(2,128)(2,1)} %all_to_all.5), kind=kLoop, calls=%fused_computation | loop fusion | flops 62914560 | bytes 83886080 | tf_op jit(solution)/shard_map/reduce_sum | solution.py:46
  1434.8 0.0 copy-start.1
  1434.8 0.0 all-reduce.5.cloned.1.call-update
  1434.8 0.0 all-reduce.7.cloned.1.call-start
  1434.9 0.0 copy-done.2
  1434.9 0.6 dynamic-slice
  1436.1 377.6 %all-reduce.5.cloned.1.call-done = f32[4194304]{0:T(1024)} async-done(((f32[4194304]{0:T(1024)}), f32[4194304]{0:T(1024)}) %all-reduce.5.cloned.1.call-update) | async-done | bytes 16777232
  1813.7 5.7 dynamic-slice.1
  1819.4 0.0 all-reduce.7.cloned.1.call-update
  1819.4 0.0 copy-done.1
  1819.5 0.6 dynamic-slice.2
  1820.7 288.0 %all-reduce.7.cloned.1.call-done = f32[2097152]{0:T(1024)} async-done(((f32[2097152]{0:T(1024)}), f32[2097152]{0:T(1024)}) %all-reduce.7.cloned.1.call-update) | async-done | bytes 8388624
  2108.7 3.0 dynamic-slice.3
  (1 shorter events, 0.0 us)
Async XLA Ops:
  6.5 1807.2 %all-reduce.5.cloned.1.call-start = ((), (), s32[]{:S(2)}) async-start(), calls=%async_computation.1 | async-start | bytes 33554432
  6.5 74.2 %slice-start = ((s8[8388608]{0:T(1024)(128)(4,1)}), s8[4194304]{0:T(1024)(128)(4,1)S(1)}, s32[]{:S(2)}) async-start(s8[8388608]{0:T(1024)(128)(4,1)} %bitcast.36), calls=%async_computation.3 | async-start | bytes 8388608
  36.9 43.8 %slice-start.1 = ((s8[8388608]{0:T(1024)(128)(4,1)}), s8[4194304]{0:T(1024)(128)(4,1)S(1)}, s32[]{:S(2)}) async-start(s8[8388608]{0:T(1024)(128)(4,1)} %bitcast.36), calls=%async_computation.4 | async-start | bytes 8388608
  36.9 43.8 %copy-start = (bf16[2048,1024]{1,0:T(8,128)(2,1)S(1)}, bf16[2048,1024]{1,0:T(8,128)(2,1)}, u32[]{:S(2)}) copy-start(bf16[2048,1024]{1,0:T(8,128)(2,1)} %param.12) | copy-start | bytes 12582916
  102.5 25.3 %copy-start.3 = (bf16[2,1024,1024]{2,1,0:T(8,128)(2,1)S(1)}, bf16[2,1024,1024]{2,1,0:T(8,128)(2,1)}, u32[]{:S(2)}) copy-start(bf16[2,1024,1024]{2,1,0:T(8,128)(2,1)} %add_convert_fusion) | copy-start | bytes 12582916
  1254.4 180.5 %copy-start.2 = (u32[32]{0:T(128)S(1)}, u32[32]{0:T(128)}, u32[]{:S(2)}) copy-start(u32[32]{0:T(128)} %constant.17) | copy-start | bytes 388
  1434.8 384.6 %copy-start.1 = (u32[32]{0:T(128)S(1)}, u32[32]{0:T(128)}, u32[]{:S(2)}) copy-start(u32[32]{0:T(128)} %constant.21) | copy-start | bytes 388
  1434.8 673.8 %all-reduce.7.cloned.1.call-start = ((), (), s32[]{:S(2)}) async-start(), calls=%async_computation.2 | async-start | bytes 16777216
Sparse Core Ops, SparseCore 0:
  1435.0 378.6 all-reduce.4
  1819.6 289.0 all-reduce.6
where the time goes:
time: 2130 us; the launch traced here: 2120 us
  blocking collectives  755 us (35%)
  waiting for transfers between devices  666 us (31%)
  other arithmetic  309 us (15%)
  matrix products  218 us (10%)
  local copies, waits for them, and re-layouts  157 us (7%)
    all_to_all x1, blocking collectives, per_device(): incoming = lax.all_to_all(outgoing, 'dx', 1, 1, tiled=True)  755 us
    unnamed x4, waiting for transfers between devices  666 us
    reduce_sum x1, other arithmetic, per_device(): part_sum = jnp.sum(incoming, axis=(0, 1), dtype=jnp.float32)  180 us
    concatenate x1, other arithmetic, local_grads(): jnp.concatenate([grad_piece.reshape(batch_count, -1) for grad_piece in (g...  128 us
    concatenate x4, local copies, waits for them, and re-layouts, local_grads(): jnp.concatenate([grad_piece.reshape(batch_count, -1) for grad_piece in (g...  104 us
    dot_general x1, matrix products, local_grads(): jnp.einsum('mtd,fd->mtf', grad_out, w_out_two, preferred_element_type=jnp...  43.8 us
  transfers between devices with their start and end apart: 2, of which 2 were waited for; matrix products, arithmetic and copies ran while one was open for 0% of the time, Pallas kernels for 0%

commit v1 on v0

v1 whole, which is shorter than its diff:
```python
import functools

import jax
import jax.numpy as jnp
from jax import lax
from jax.experimental import pallas as pl
from jax.experimental.pallas import tpu as pltpu
from jax.sharding import PartitionSpec as P

MESH = pl.DeviceIdType.MESH
F32 = jnp.float32
BF16 = jnp.bfloat16
N_CHUNK = 8
ROOT = 0.7978845608028654
CUBE = 0.044715


def gelu_hidden(pre):
    square = pre * pre
    bend = jnp.tanh(pre * (ROOT + (ROOT * CUBE) * square))
    half = 0.5 * pre
    return half + half * bend


def gelu_slope(pre):
    square = pre * pre
    bend = jnp.tanh(pre * (ROOT + (ROOT * CUBE) * square))
    tail = ((1.0 - bend * bend) * pre) * ((1.5 * ROOT * CUBE) * square + 0.5 * ROOT)
    return (0.5 + 0.5 * bend) + tail


def dot_nn(left, right):
    return lax.dot_general(left, right, (((1,), (0,)), ((), ())), preferred_element_type=F32)


def dot_nt(left, right):
    return lax.dot_general(left, right, (((1,), (1,)), ((), ())), preferred_element_type=F32)


class Dims:
    def __init__(self, tokens, width):
        self.tokens = tokens
        self.micro = tokens // 2
        self.width = width
        self.hidden = 4 * width
        self.rows = width // 8
        self.tile = 2 * self.rows
        self.half = width // 2
        unit = self.rows // 16
        self.row_a = max(8, (unit * 5) // 8 * 8)
        self.row_c = 4 * unit
        self.row_b = self.rows - self.row_a - self.row_c
        self.block = min(256, self.micro)
        self.span = min(512, width)


def kernel(dims, z2, z1, x2, x1, dy, win2, wo1, wo2, out,
           gin, xt, acc, dz, zbuf, wbuf, winbuf, ht, stage, rcore,
           s1, r1a, r1b, r1c, s2a, s2b, s2c, r2a, r2b, r2c, s3ab, s3c, r3ab, r3c, s4ab, s4c, r4ab, r4c, fin,
           zsem, wsem, winsem, xsem, gsem,
           core_send, core_recv, send1, recv1, send2, recv2, send3, recv3, send4, recv4,
           fin_send, fin_recv, fin_local, credit):
    rows, tile, width, half = dims.rows, dims.tile, dims.width, dims.half
    micro, tokens, block, span = dims.micro, dims.tokens, dims.block, dims.span
    row_a, row_b, row_c = dims.row_a, dims.row_b, dims.row_c
    row_ab = row_a + row_b
    iz, iy, ix = lax.axis_index('dz'), lax.axis_index('dy'), lax.axis_index('dx')
    px, core = ix // 2, ix % 2
    zhi, zlo = iz // 2, iz % 2
    to_core = (iz, iy, px * 2 + (1 - core))
    to_x = (iz, iy, (1 - px) * 2 + core)
    to_xc = (iz, iy, (1 - px) * 2 + (1 - core))
    to_y = (iz, 1 - iy, ix)
    to_za = (zhi * 2 + (1 - zlo), iy, ix)
    to_zb = ((1 - zhi) * 2 + zlo, iy, ix)
    keep_x = pl.ds(pl.multiple_of(px * half, 128), half)
    send_x = pl.ds(pl.multiple_of((1 - px) * half, 128), half)
    CORE, A1, B1, C1, A2, B2, C2, AB3, C3, AB4, C4 = range(11)

    barrier = pltpu.get_barrier_semaphore()
    for peer in (to_core, to_x, to_xc, to_y, to_za, to_zb):
        pl.semaphore_signal(barrier, inc=1, device_id=peer, device_id_type=MESH)

    def piece_start(num):
        k, s, p = num // 8, (num // 4) % 2, num % 4
        b, i, g = k // 4, (k // 2) % 2, k % 2
        j = 2 * i + jnp.where(s == 0, 1 - core, core)
        slot = num % 3

        def from_block(zref, wref):
            @pl.when(g == 0)
            def _():
                for h in range(2):
                    col = pl.multiple_of((dims.hidden // 8) * (2 * p + h) + rows * j, rows)
                    pltpu.make_async_copy(zref.at[:, pl.ds(col, rows)], zbuf.at[slot, :, pl.ds(h * rows, rows)], zsem.at[slot]).start()

            @pl.when(g == 1)
            def _():
                col = pl.multiple_of(width * j + tile * p, tile)
                pltpu.make_async_copy(zref.at[:, pl.ds(col, tile)], zbuf.at[slot], zsem.at[slot]).start()
                pltpu.make_async_copy(wref.at[pl.ds(col, tile), :], wbuf.at[slot], wsem.at[slot]).start()

        @pl.when(b == 0)
        def _():
            from_block(z2, wo2)

        @pl.when(b == 1)
        def _():
            from_block(z1, wo1)

    def piece_wait(num, with_w):
        slot = num % 3
        pltpu.make_async_copy(z2.at[:, pl.ds(0, tile)], zbuf.at[slot], zsem.at[slot]).wait()
        if with_w:
            pltpu.make_async_copy(wo2.at[pl.ds(0, tile), :], wbuf.at[slot], wsem.at[slot]).wait()

    def x_copy(xref):
        return pltpu.make_async_copy(xref, dz, xsem)

    def core_copy(p):
        return pltpu.make_async_remote_copy(stage.at[p % 2], rcore.at[p], core_send.at[p % 2], core_recv.at[p], device_id=to_core, device_id_type=MESH)

    def phase1(slot):
        return (
            pltpu.make_async_remote_copy(s1.at[slot, :, :, :, pl.ds(0, row_a), send_x], r1a.at[slot], send1.at[slot, 0], recv1.at[slot, 0], device_id=to_x, device_id_type=MESH),
            pltpu.make_async_remote_copy(s1.at[slot, 1 - iy, :, :, pl.ds(row_a, row_b), :], r1b.at[slot], send1.at[slot, 1], recv1.at[slot, 1], device_id=to_y, device_id_type=MESH),
            pltpu.make_async_remote_copy(s1.at[slot, :, :, 1 - zlo, pl.ds(row_ab, row_c), :], r1c.at[slot], send1.at[slot, 2], recv1.at[slot, 2], device_id=to_za, device_id_type=MESH),
        )

    def phase2():
        return (
            pltpu.make_async_remote_copy(s2a.at[1 - iy], r2a, send2.at[0], recv2.at[0], device_id=to_y, device_id_type=MESH),
            pltpu.make_async_remote_copy(s2b.at[:, :, :, send_x], r2b, send2.at[1], recv2.at[1], device_id=to_x, device_id_type=MESH),
            pltpu.make_async_remote_copy(s2c.at[:, 1 - zhi], r2c, send2.at[2], recv2.at[2], device_id=to_zb, device_id_type=MESH),
        )

    def phase3():
        return (
            pltpu.make_async_remote_copy(s3ab.at[:, 1 - zlo], r3ab, send3.at[0], recv3.at[0], device_id=to_za, device_id_type=MESH),
            pltpu.make_async_remote_copy(s3c.at[:, :, send_x], r3c, send3.at[1], recv3.at[1], device_id=to_x, device_id_type=MESH),
        )

    def phase4():
        return (
            pltpu.make_async_remote_copy(s4ab.at[1 - zhi], r4ab, send4.at[0], recv4.at[0], device_id=to_zb, device_id_type=MESH),
            pltpu.make_async_remote_copy(s4c.at[1 - iy], r4c, send4.at[1], recv4.at[1], device_id=to_y, device_id_type=MESH),
        )

    def grant(kind, peer, ok):
        @pl.when(ok)
        def _():
            pl.semaphore_signal(credit.at[kind], inc=1, device_id=peer, device_id_type=MESH)

    def claim(kind, ok):
        @pl.when(ok)
        def _():
            pl.semaphore_wait(credit.at[kind], 1)

    def out_place(i, c, x):
        return out.at[2 * i + c, :, pl.ds(pl.multiple_of(x * half, 128), half)]

    def fin_remote(chunk):
        b, i, g = chunk // 4, (chunk // 2) % 2, chunk % 2
        return pltpu.make_async_remote_copy(fin, out_place(i, core, px), fin_send, fin_recv.at[i, ix], device_id=(iz, iy, 2 * b + g), device_id_type=MESH)

    def fin_here(chunk):
        i = (chunk // 2) % 2
        return pltpu.make_async_copy(fin, out_place(i, core, px), fin_local)

    def owner_of(chunk):
        return 2 * (chunk // 4) + chunk % 2

    def fin_wait(chunk):
        @pl.when(owner_of(chunk) == ix)
        def _():
            fin_here(chunk).wait()

        @pl.when(owner_of(chunk) != ix)
        def _():
            fin_remote(chunk).wait_send()

    def service(k):
        @pl.when(jnp.logical_and(k >= 4, k < N_CHUNK + 4))
        def _():
            chunk = k - 4
            more = chunk < N_CHUNK - 1
            ab, c = phase4()

            @pl.when(chunk >= 1)
            def _():
                fin_wait(chunk - 1)
            ab.wait()
            fin[0:row_ab, :] = s4ab[zhi] + r4ab[...]
            grant(AB4, to_zb, more)
            c.wait()
            fin[row_ab:rows, :] = s4c[iy] + r4c[...]
            grant(C4, to_y, more)

            @pl.when(owner_of(chunk) == ix)
            def _():
                fin_here(chunk).start()

            @pl.when(owner_of(chunk) != ix)
            def _():
                fin_remote(chunk).start()

        @pl.when(jnp.logical_and(k >= 3, k < N_CHUNK + 3))
        def _():
            chunk = k - 3
            more, later = chunk < N_CHUNK - 1, chunk >= 1
            ab, c = phase3()
            ab4, c4 = phase4()
            ab.wait()
            s4ab[...] = s3ab[:, zlo] + r3ab[...]
            grant(AB3, to_za, more)
            claim(AB4, later)
            ab4.start()
            c.wait()
            s4c[...] = s3c[:, :, keep_x] + r3c[...]
            grant(C3, to_x, more)
            claim(C4, later)
            c4.start()

        @pl.when(jnp.logical_and(k >= 2, k < N_CHUNK + 2))
        def _():
            chunk = k - 2
            more, later = chunk < N_CHUNK - 1, chunk >= 1
            a, b, c = phase2()
            ab3, c3 = phase3()
            a.wait()
            s3ab[:, :, 0:row_a, :] = s2a[iy] + r2a[...]
            grant(A2, to_y, more)
            b.wait()
            s3ab[:, :, row_a:row_ab, :] = s2b[:, :, :, keep_x] + r2b[...]
            grant(B2, to_x, more)
            claim(AB3, later)
            ab3.start()
            c.wait()
            s3c[...] = s2c[:, zhi] + r2c[...]
            grant(C2, to_zb, more)
            claim(C3, later)
            c3.start()

        @pl.when(jnp.logical_and(k >= 1, k < N_CHUNK + 1))
        def _():
            chunk = k - 1
            slot = chunk % 2
            more, later = chunk < N_CHUNK - 2, chunk >= 1
            a, b, c = phase1(slot)
            a2, b2, c2 = phase2()
            a.wait()
            s2a[...] = s1[slot, :, :, :, 0:row_a, keep_x] + r1a[slot]
            grant(A1, to_x, more)
            claim(A2, later)
            a2.start()
            b.wait()
            s2b[...] = s1[slot, iy, :, :, row_a:row_ab, :] + r1b[slot]
            grant(B1, to_y, more)
            claim(B2, later)
            b2.start()
            c.wait()
            s2c[...] = s1[slot, :, :, zlo, row_ab:rows, :] + r1c[slot]
            grant(C1, to_za, more)
            claim(C2, later)
            c2.start()

    def emit_tile(k, s, p, cols, value):
        @pl.when(s == 0)
        def _():
            stage[p % 2, :, cols] = value

        @pl.when(s == 1)
        def _():
            total = value + rcore[p, :, cols]
            s1[k % 2, p // 2, p % 2, 0, :, cols] = total[0:rows]
            s1[k % 2, p // 2, p % 2, 1, :, cols] = total[rows:tile]

    def tile_open(k, s, p):
        @pl.when(s == 0)
        def _():
            @pl.when(p >= 2)
            def _():
                core_copy(p - 2).wait_send()

        @pl.when(s == 1)
        def _():
            core_copy(p).wait_recv()

    def tile_close(k, s, p):
        @pl.when(s == 0)
        def _():
            claim(CORE, k >= 1)
            core_copy(p).start()

        @pl.when(s == 1)
        def _():
            grant(CORE, to_core, k < N_CHUNK - 1)

    def drain_stage(s):
        @pl.when(s == 0)
        def _():
            core_copy(2).wait_send()
            core_copy(3).wait_send()

    def half_out(k, s):
        @pl.loop(0, 4)
        def _(p):
            num = k * 8 + s * 4 + p

            @pl.when(num + 2 < 64)
            def _():
                piece_start(num + 2)
            piece_wait(num, False)
            slot = num % 3
            for r in range(tokens // block):
                pre = zbuf[slot, r * block:(r + 1) * block, :].astype(F32)
                ht[:, r * block:(r + 1) * block] = gelu_hidden(pre).astype(BF16).T
            tile_open(k, s, p)
            for n in range(width // span):
                cols = slice(n * span, (n + 1) * span)
                value = None
                for m in range(2):
                    part = dot_nn(ht[:, m * micro:(m + 1) * micro], gin[m * micro:(m + 1) * micro, cols]).astype(BF16).astype(F32)
                    value = part if value is None else value + part
                emit_tile(k, s, p, cols, value)
            tile_close(k, s, p)
        drain_stage(s)

    def half_in(k, s):
        b, i = k // 4, (k // 2) % 2
        j = 2 * i + jnp.where(s == 0, 1 - core, core)

        @pl.when(b == 0)
        def _():
            pltpu.make_async_copy(win2.at[:, pl.ds(pl.multiple_of(width * j, width), width)], winbuf, winsem).start()

        @pl.loop(0, 4)
        def _(p):
            num = k * 8 + s * 4 + p

            @pl.when(num + 2 < 64)
            def _():
                piece_start(num + 2)
            piece_wait(num, True)
            slot = num % 3
            where = pl.ds(pl.multiple_of(p * tile, tile), tile)
            for r in range(tokens // block):
                part = slice(r * block, (r + 1) * block)
                back = dot_nt(gin[part, :], wbuf[slot])
                dz[part, where] = (back * gelu_slope(zbuf[slot, part, :].astype(F32))).astype(BF16)

        @pl.loop(0, 4)
        def _(p):
            lines = pl.ds(pl.multiple_of(p * tile, tile), tile)
            tile_open(k, s, p)
            for n in range(width // span):
                cols = slice(n * span, (n + 1) * span)
                value = None
                for m in range(2):
                    part = dot_nn(xt[lines, m * micro:(m + 1) * micro], dz[m * micro:(m + 1) * micro, cols]).astype(BF16).astype(F32)
                    value = part if value is None else value + part
                emit_tile(k, s, p, cols, value)
            tile_close(k, s, p)
        drain_stage(s)

    def pass_back(k):
        @pl.when(k // 4 == 0)
        def _():
            pltpu.make_async_copy(win2.at[:, pl.ds(0, width)], winbuf, winsem).wait()

            @pl.loop(0, width // tile)
            def _(n):
                lines = pl.ds(pl.multiple_of(n * tile, tile), tile)
                for m in range(2):
                    part = slice(m * micro, (m + 1) * micro)
                    acc[part, lines] += dot_nt(dz[part, :], winbuf[lines, :])

    piece_start(0)
    first = pltpu.make_async_copy(dy, gin, gsem)
    first.start()
    piece_start(1)
    x_copy(x2).start()
    first.wait()

    @pl.loop(0, tokens // block)
    def _(r):
        part = pl.ds(pl.multiple_of(r * block, block), block)
        acc[part, :] = gin[part, :].astype(F32)
    pl.semaphore_wait(barrier, 6)

    @pl.loop(0, N_CHUNK + 4)
    def _(k):
        @pl.when(k < N_CHUNK)
        def _():
            @pl.when(k == 4)
            def _():
                x_copy(x1).start()

                @pl.loop(0, tokens // block)
                def _(r):
                    part = pl.ds(pl.multiple_of(r * block, block), block)
                    gin[part, :] = acc[part, :].astype(BF16)

            @pl.when(k % 2 == 0)
            def _():
                @pl.loop(0, 2)
                def _(s):
                    half_out(k, s)

            @pl.when(k % 4 == 1)
            def _():
                x_copy(x2).wait()

                @pl.loop(0, tokens // block)
                def _(r):
                    part = pl.ds(pl.multiple_of(r * block, block), block)
                    for q in range(width // tile):
                        xt[q * tile:(q + 1) * tile, part] = dz[part, q * tile:(q + 1) * tile].T

            @pl.when(k % 2 == 1)
            def _():
                half_in(k, 0)
                pass_back(k)
                half_in(k, 1)

            claim(A1, k >= 2)
            claim(B1, k >= 2)
            claim(C1, k >= 2)
            for copy in phase1(k % 2):
                copy.start()

            @pl.when(k % 2 == 1)
            def _():
                pass_back(k)
        service(k)

    fin_wait(N_CHUNK - 1)
    for i in range(2):
        for d in range(4):
            @pl.when(ix != d)
            def _():
                place = out_place(i, d % 2, d // 2)
                pltpu.make_async_remote_copy(fin, place, fin_send, fin_recv.at[i, d], device_id=to_core, device_id_type=MESH).wait_recv()


def scratch(dims):
    t, w, r, h = dims.tokens, dims.width, dims.rows, dims.half
    a, b, c = dims.row_a, dims.row_b, dims.row_c
    tile = dims.tile
    V, DMA = pltpu.VMEM, pltpu.SemaphoreType.DMA
    return [
        V((t, w), BF16), V((w, t), BF16), V((t, w), F32), V((t, w), BF16), V((3, t, tile), BF16), V((3, tile, w), BF16), V((w, w), BF16),
        V((tile, t), BF16), V((2, tile, w), F32), V((4, tile, w), F32),
        V((2, 2, 2, 2, r, w), F32), V((2, 2, 2, 2, a, h), F32), V((2, 2, 2, b, w), F32), V((2, 2, 2, c, w), F32),
        V((2, 2, 2, a, h), F32), V((2, 2, b, w), F32), V((2, 2, c, w), F32),
        V((2, 2, a, h), F32), V((2, 2, b, h), F32), V((2, c, w), F32),
        V((2, 2, a + b, h), F32), V((2, c, w), F32), V((2, a + b, h), F32), V((2, c, h), F32),
        V((2, a + b, h), F32), V((2, c, h), F32), V((a + b, h), F32), V((c, h), F32), V((r, h), F32),
        DMA((3,)), DMA((3,)), DMA, DMA, DMA,
        DMA((2,)), DMA((4,)), DMA((2, 3)), DMA((2, 3)), DMA((3,)), DMA((3,)), DMA((2,)), DMA((2,)), DMA((2,)), DMA((2,)),
        DMA, DMA((2, 4)), DMA, pltpu.SemaphoreType.REGULAR((11,)),
    ]


def solution(mesh):
    row_spec = P(('dz', 'dy', 'dx'), None)
    full_spec = P(None, None)

    def per_device(act_one, pre_one, act_two, pre_two, grad_out, w_in_two, w_out_one, w_out_two):
        dims = Dims(*grad_out.shape)
        any_spec = pl.BlockSpec(memory_space=pl.ANY)
        shards = pl.pallas_call(
            functools.partial(kernel, dims),
            out_shape=jax.ShapeDtypeStruct((4, dims.rows, dims.width), F32),
            in_specs=[any_spec] * 8,
            out_specs=any_spec,
            scratch_shapes=scratch(dims),
            compiler_params=pltpu.CompilerParams(collective_id=0, has_side_effects=True, vmem_limit_bytes=67043328),
        )(pre_two, pre_one, act_two, act_one, grad_out, w_in_two, w_out_one, w_out_two)
        across = jnp.transpose(shards, (1, 0, 2)).reshape(-1)
        return jnp.where(lax.axis_index('dx') % 2 == 0, shards.reshape(-1), across)

    return jax.shard_map(per_device, mesh=mesh, in_specs=(row_spec,) * 5 + (full_spec,) * 3, out_specs=P(('dx', 'dy', 'dz')), check_vma=False)
```

time: 2130 us -> 340 us (0.16)
  blocking collectives: 755 us -> 0 us
  waiting for transfers between devices: 666 us -> 0 us
  Pallas kernels: 0 us -> 335 us
  other arithmetic: 309 us -> 1.54 us
  matrix products: 218 us -> 0 us
  local copies, waits for them, and re-layouts: 157 us -> 3.74 us
    all_to_all x1 -> x0, blocking collectives: 755 us -> none  [per_device(): incoming = lax.all_to_all(outgoing, 'dx', 1, 1, tiled=True)]
    unnamed x4 -> x0, waiting for transfers between devices: 666 us -> none
    pallas_call x0 -> x1, Pallas kernels: none -> 335 us  [per_device(): pl.pallas_call(functools.partial(kernel, dims), out_shape=jax.ShapeDtypeS...]
    dot_general x7 -> x0, matrix products: 218 us -> none  [the longest x1 43.8 us: local_grads(): jnp.einsum('mtd,fd->mtf', grad_out, w_out_two, preferred_element_type=jnp...]
    reduce_sum x1 -> x0, other arithmetic: 180 us -> none  [per_device(): part_sum = jnp.sum(incoming, axis=(0, 1), dtype=jnp.float32)]
    concatenate x1 -> x0, other arithmetic: 128 us -> none  [local_grads(): jnp.concatenate([grad_piece.reshape(batch_count, -1) for grad_piece in (g...]
    concatenate x4 -> x0, local copies, waits for them, and re-layouts: 104 us -> none  [local_grads(): jnp.concatenate([grad_piece.reshape(batch_count, -1) for grad_piece in (g...]
    convert_element_type x2 -> x0, local copies, waits for them, and re-layouts: 42.8 us -> none  [the longest x1 21.6 us: local_grads(): jnp.einsum('mtd,mtf->mdf', act_one, d_pre_one, preferred_element_type=jnp...]
  transfers between devices with their start and end apart: 2 -> 0, of which waited for: 2 -> 0; matrix products, arithmetic and copies ran while one was open for 0% -> 0% of each run, Pallas kernels for 0% -> 0%
where the time goes in v1:
time: 340 us
  Pallas kernels  335 us (99%)
  local copies, waits for them, and re-layouts  3.74 us (1%)
    pallas_call x1, Pallas kernels, per_device(): pl.pallas_call(functools.partial(kernel, dims), out_shape=jax.ShapeDtypeS...  335 us

profile of v1, /device:TPU:0, one launch (start us, length us, event | category | flops | bytes accessed | tf_op | source)
XLA Modules:
  0.0 340.3 jit_solution(7686569786592727824)
XLA Ops:
  0.0 335.0 %shard_map.82 = f32[4,128,1024]{2,1,0:T(8,128)} custom-call(bf16[2048,4096]{1,0:T(8,128)(2,1)} %z2.1, bf16[2048,4096]{1,0:T(8,128)(2,1)} %z1.1, bf16[2048,1024]{1,0:T(8,128)(2,1)} %x2.1, bf16[2048,1024]{1,0:T(8,128)(2,1)} %x1.1, bf16[2048,1024]{1,0:T(8,128)(2,1)} %dy.1, bf16[1024,4096]{1,0:T(8,128)(2,1)} %win2.1, bf16[4096,1024]{1,0:T(8,128)(2,1)} %wo1.1, ...), custom_call_target="tpu_custom_call" | custom-call | tf_op jit(solution)/shard_map/pallas_call | solution.py:472
  335.0 0.0 copy-start
  335.0 2.2 copy.10
  337.2 0.0 copy-done
  337.2 1.4 copy.13
  338.6 0.2 copy.11
  338.8 1.5 broadcast_select_fusion
Async XLA Ops:
  335.0 2.2 copy-start

commit v2 on v1

v2 whole, which is shorter than its diff:
```python
import functools

import jax
import jax.numpy as jnp
from jax import lax
from jax.experimental import pallas as pl
from jax.experimental.pallas import tpu as pltpu
from jax.sharding import PartitionSpec as P

MESH = pl.DeviceIdType.MESH
F32 = jnp.float32
BF16 = jnp.bfloat16
N_CHUNK = 8
GRANULES = 2 * N_CHUNK
FIRST, LAG = 2, 2
ROOT = 0.7978845608028654
CUBE = 0.044715


def gelu_hidden(pre):
    square = pre * pre
    bend = jnp.tanh(pre * (ROOT + (ROOT * CUBE) * square))
    half = 0.5 * pre
    return half + half * bend


def gelu_slope(pre):
    square = pre * pre
    bend = jnp.tanh(pre * (ROOT + (ROOT * CUBE) * square))
    tail = ((1.0 - bend * bend) * pre) * ((1.5 * ROOT * CUBE) * square + 0.5 * ROOT)
    return (0.5 + 0.5 * bend) + tail


def dot_nn(left, right):
    return lax.dot_general(left, right, (((1,), (0,)), ((), ())), preferred_element_type=F32)


def dot_nt(left, right):
    return lax.dot_general(left, right, (((1,), (1,)), ((), ())), preferred_element_type=F32)


class Dims:
    def __init__(self, tokens, width):
        self.tokens = tokens
        self.micro = tokens // 2
        self.width = width
        self.hidden = 4 * width
        self.rows = width // 8
        self.tile = 2 * self.rows
        self.half = width // 2
        self.quarter = width // 4
        unit = self.rows // 16
        self.row_a = max(8, (unit * 5) // 8 * 8)
        self.row_c = 4 * unit
        self.row_b = self.rows - self.row_a - self.row_c
        self.block = min(256, self.micro)
        self.span = min(512, width)


def kernel(dims, z2, z1, x2, x1, dy, win2, wo1, wo2, out,
           gin, xt, acc, dz, zbuf, wbuf, winbuf, ht, stage, rcore,
           s1, r1a, r1b, r1c, s2a, s2b, s2c, r2a, r2b, r2c, s3ab, s3c, r3ab, r3c, s4ab, s4c, r4ab, r4c, fin,
           zsem, wsem, winsem, xsem, gsem,
           core_send, core_recv, send1, recv1, send2, recv2, send3, recv3, send4, recv4,
           fin_send, fin_recv, fin_local, credit):
    rows, tile, width, half, quarter = dims.rows, dims.tile, dims.width, dims.half, dims.quarter
    micro, tokens, block, span = dims.micro, dims.tokens, dims.block, dims.span
    row_a, row_b, row_c = dims.row_a, dims.row_b, dims.row_c
    row_ab = row_a + row_b
    lanes = 128
    iz, iy, ix = lax.axis_index('dz'), lax.axis_index('dy'), lax.axis_index('dx')
    px, core = ix // 2, ix % 2
    zhi, zlo = iz // 2, iz % 2
    to_core = (iz, iy, px * 2 + (1 - core))
    to_x = (iz, iy, (1 - px) * 2 + core)
    to_xc = (iz, iy, (1 - px) * 2 + (1 - core))
    to_y = (iz, 1 - iy, ix)
    to_za = (zhi * 2 + (1 - zlo), iy, ix)
    to_zb = ((1 - zhi) * 2 + zlo, iy, ix)
    keep_x = pl.ds(pl.multiple_of(px * quarter, min(quarter, lanes)), quarter)
    send_x = pl.ds(pl.multiple_of((1 - px) * quarter, min(quarter, lanes)), quarter)
    CORE, A1, B1, C1, A2, B2, C2, AB3, C3, AB4, C4 = range(11)

    barrier = pltpu.get_barrier_semaphore()
    for peer in (to_core, to_x, to_xc, to_y, to_za, to_zb):
        pl.semaphore_signal(barrier, inc=1, device_id=peer, device_id_type=MESH)

    def order(num):
        k, t = num // 8, num % 8
        b, i, g = k // 4, (k // 2) % 2, k % 2
        plain_s, plain_p = t // 4, t % 4
        first = jnp.logical_or(t == 0, jnp.logical_and(t % 2 == 1, t < 7))
        mixed_s = jnp.where(first, 0, 1)
        mixed_p = jnp.where(first, (t + 1) // 2, jnp.where(t == 7, 3, t // 2 - 1))
        s = jnp.where(g == 0, mixed_s, plain_s)
        p = jnp.where(g == 0, mixed_p, plain_p)
        return k, b, i, g, s, p

    def piece_start(num):
        k, b, i, g, s, p = order(num)
        j = 2 * i + jnp.where(s == 0, 1 - core, core)
        slot = num % 3

        def from_block(zref, wref):
            @pl.when(g == 0)
            def _():
                for h in range(2):
                    col = pl.multiple_of((dims.hidden // 8) * (2 * p + h) + rows * j, rows)
                    pltpu.make_async_copy(zref.at[:, pl.ds(col, rows)], zbuf.at[slot, :, pl.ds(h * rows, rows)], zsem.at[slot]).start()

            @pl.when(g == 1)
            def _():
                col = pl.multiple_of(width * j + tile * p, tile)
                pltpu.make_async_copy(zref.at[:, pl.ds(col, tile)], zbuf.at[slot], zsem.at[slot]).start()
                pltpu.make_async_copy(wref.at[pl.ds(col, tile), :], wbuf.at[slot], wsem.at[slot]).start()

        @pl.when(b == 0)
        def _():
            from_block(z2, wo2)

        @pl.when(b == 1)
        def _():
            from_block(z1, wo1)

    def piece_ahead(num):
        @pl.when(num + 2 < 8 * N_CHUNK)
        def _():
            piece_start(num + 2)

    def z_wait(num):
        pltpu.make_async_copy(z2.at[:, pl.ds(0, tile)], zbuf.at[num % 3], zsem.at[num % 3]).wait()

    def w_wait(num):
        pltpu.make_async_copy(wo2.at[pl.ds(0, tile), :], wbuf.at[num % 3], wsem.at[num % 3]).wait()

    def x_copy(xref):
        return pltpu.make_async_copy(xref, dz, xsem)

    def core_copy(p):
        return pltpu.make_async_remote_copy(stage.at[p % 2], rcore.at[p], core_send.at[p % 2], core_recv.at[p], device_id=to_core, device_id_type=MESH)

    def remote(src, dst, sends, recvs, peer):
        return pltpu.make_async_remote_copy(src, dst, sends, recvs, device_id=peer, device_id_type=MESH)

    def shift(q, part, size):
        return pl.ds(pl.multiple_of((q % 2) * half + part, min(quarter, lanes)), size)

    def phase1(q):
        slot, r = (q // 2) % 2, q % 4
        return (
            remote(s1.at[slot, :, :, :, pl.ds(0, row_a), shift(q, (1 - px) * quarter, quarter)], r1a.at[r], send1.at[r, 0], recv1.at[r, 0], to_x),
            remote(s1.at[slot, 1 - iy, :, :, pl.ds(row_a, row_b), shift(q, 0, half)], r1b.at[r], send1.at[r, 1], recv1.at[r, 1], to_y),
            remote(s1.at[slot, :, :, 1 - zlo, pl.ds(row_ab, row_c), shift(q, 0, half)], r1c.at[r], send1.at[r, 2], recv1.at[r, 2], to_za),
        )

    def phase1_early(q, p):
        slot, r = (q // 2) % 2, q % 4
        ty, tz = p // 2, p % 2
        remote(s1.at[slot, ty, tz, :, pl.ds(0, row_a), shift(q, (1 - px) * quarter, quarter)], r1a.at[r, ty, tz], send1.at[r, 0], recv1.at[r, 0], to_x).start()
        remote(s1.at[slot, ty, tz, 1 - zlo, pl.ds(row_ab, row_c), shift(q, 0, half)], r1c.at[r, ty, tz], send1.at[r, 2], recv1.at[r, 2], to_za).start()

        @pl.when(ty != iy)
        def _():
            remote(s1.at[slot, ty, tz, :, pl.ds(row_a, row_b), shift(q, 0, half)], r1b.at[r, tz], send1.at[r, 1], recv1.at[r, 1], to_y).start()

    def phase2(q):
        r, v = q % 4, q % 2
        return (
            remote(s2a.at[v, 1 - iy], r2a.at[r], send2.at[r, 0], recv2.at[r, 0], to_y),
            remote(s2b.at[v, :, :, :, send_x], r2b.at[r], send2.at[r, 1], recv2.at[r, 1], to_x),
            remote(s2c.at[v, :, 1 - zhi], r2c.at[r], send2.at[r, 2], recv2.at[r, 2], to_zb),
        )

    def phase3(q):
        r, v = q % 4, q % 2
        return (
            remote(s3ab.at[v, :, 1 - zlo], r3ab.at[r], send3.at[r, 0], recv3.at[r, 0], to_za),
            remote(s3c.at[v, :, :, send_x], r3c.at[r], send3.at[r, 1], recv3.at[r, 1], to_x),
        )

    def phase4(q):
        r, v = q % 4, q % 2
        return (
            remote(s4ab.at[v, 1 - zhi], r4ab.at[r], send4.at[r, 0], recv4.at[r, 0], to_zb),
            remote(s4c.at[v, 1 - iy], r4c.at[r], send4.at[r, 1], recv4.at[r, 1], to_y),
        )

    def grant(kind, peer, ok):
        @pl.when(ok)
        def _():
            pl.semaphore_signal(credit.at[kind], inc=1, device_id=peer, device_id_type=MESH)

    def claim(kind, ok):
        @pl.when(ok)
        def _():
            pl.semaphore_wait(credit.at[kind], 1)

    def out_place(q, n):
        i, h = (q // 4) % 2, q % 2
        j = 2 * i + core
        strip = (width // lanes // 2) * h + (width // lanes // 4) * px + n
        return (
            out.at[pl.ds(pl.multiple_of(j * rows, rows), rows), strip, :],
            out.reshape(rows, 4, width // lanes, lanes).at[:, j, strip, :],
        )

    def owner_of(q):
        return 2 * (q // 8) + (q // 2) % 2

    def fin_start(q):
        f = q % 2
        for g in range(2):
            @pl.when((q // 2) % 2 == g)
            def _():
                for n in range(quarter // lanes):
                    strip = fin.at[f, :, pl.ds(n * lanes, lanes)]
                    place = out_place(q, n)[g]

                    @pl.when(owner_of(q) == ix)
                    def _():
                        pltpu.make_async_copy(strip, place, fin_local.at[f]).start()

                    @pl.when(owner_of(q) != ix)
                    def _():
                        remote(strip, place, fin_send.at[f], fin_recv.at[(q // 4) % 2, q % 2, ix], (iz, iy, owner_of(q))).start()

    def fin_wait(q):
        f = q % 2

        @pl.when(owner_of(q) == ix)
        def _():
            pltpu.make_async_copy(fin.at[f], fin.at[f], fin_local.at[f]).wait()

        @pl.when(owner_of(q) != ix)
        def _():
            remote(fin.at[f], fin.at[f], fin_send.at[f], fin_recv.at[0, 0, ix], to_core).wait_send()

    def service(step):
        def stage_of(phase, act):
            q = step - (FIRST + LAG * (phase - 1))

            @pl.when(jnp.logical_and(q >= 0, q < GRANULES))
            def _():
                act(q, q % 4, q % 2, q < GRANULES - 4, q >= 4)

        def take4(q, r, v, more, later):
            ab, c = phase4(q)

            @pl.when(q >= 2)
            def _():
                fin_wait(q - 2)
            ab.wait()
            fin[v, 0:row_ab, :] = s4ab[v, zhi] + r4ab[r]
            grant(AB4, to_zb, more)
            c.wait()
            fin[v, row_ab:rows, :] = s4c[v, iy] + r4c[r]
            grant(C4, to_y, more)
            fin_start(q)

        def take3(q, r, v, more, later):
            ab, c = phase3(q)
            ab4, c4 = phase4(q)
            ab.wait()
            s4ab[v] = s3ab[v, :, zlo] + r3ab[r]
            grant(AB3, to_za, more)
            claim(AB4, later)
            ab4.start()
            c.wait()
            s4c[v] = s3c[v, :, :, keep_x] + r3c[r]
            grant(C3, to_x, more)
            claim(C4, later)
            c4.start()

        def take2(q, r, v, more, later):
            a, b, c = phase2(q)
            ab3, c3 = phase3(q)
            a.wait()
            s3ab[v, :, :, 0:row_a, :] = s2a[v, iy] + r2a[r]
            grant(A2, to_y, more)
            b.wait()
            s3ab[v, :, :, row_a:row_ab, :] = s2b[v, :, :, :, keep_x] + r2b[r]
            grant(B2, to_x, more)
            claim(AB3, later)
            ab3.start()
            c.wait()
            s3c[v] = s2c[v, :, zhi] + r2c[r]
            grant(C2, to_zb, more)
            claim(C3, later)
            c3.start()

        def take1(q, r, v, more, later):
            slot = (q // 2) % 2
            a, b, c = phase1(q)
            a2, b2, c2 = phase2(q)
            a.wait()
            s2a[v] = s1[slot, :, :, :, 0:row_a, shift(q, px * quarter, quarter)] + r1a[r]
            grant(A1, to_x, more)
            claim(A2, later)
            a2.start()
            b.wait()
            s2b[v] = s1[slot, iy, :, :, row_a:row_ab, shift(q, 0, half)] + r1b[r]
            grant(B1, to_y, more)
            claim(B2, later)
            b2.start()
            c.wait()
            s2c[v] = s1[slot, :, :, zlo, row_ab:rows, shift(q, 0, half)] + r1c[r]
            grant(C1, to_za, more)
            claim(C2, later)
            c2.start()

        stage_of(4, take4)
        stage_of(3, take3)
        stage_of(2, take2)
        stage_of(1, take1)

    def emit_tile(k, s, p, cols, value):
        @pl.when(s == 0)
        def _():
            stage[p % 2, :, cols] = value

        @pl.when(s == 1)
        def _():
            total = value + rcore[p, :, cols]
            s1[k % 2, p // 2, p % 2, 0, :, cols] = total[0:rows]
            s1[k % 2, p // 2, p % 2, 1, :, cols] = total[rows:tile]

    def tile_open(k, s, p):
        @pl.when(s == 0)
        def _():
            @pl.when(jnp.logical_or(k >= 1, p >= 2))
            def _():
                core_copy(p).wait_send()

        @pl.when(s == 1)
        def _():
            core_copy(p).wait_recv()

    def tile_close(k, s, p):
        @pl.when(s == 0)
        def _():
            claim(CORE, k >= 1)
            core_copy(p).start()

        @pl.when(s == 1)
        def _():
            grant(CORE, to_core, k < N_CHUNK - 1)

            @pl.when(k == 0)
            def _():
                for q in range(2):
                    phase1_early(q, p)

    def hidden_block(num, side, r):
        part = slice(r * block, (r + 1) * block)
        ht[side, :, part] = gelu_hidden(zbuf[num % 3, part, :].astype(F32)).astype(BF16).T

    def product(left, right, cols):
        value = None
        for m in range(2):
            part = slice(m * micro, (m + 1) * micro)
            term = dot_nn(left(part), right(part, cols)).astype(BF16).astype(F32)
            value = term if value is None else value + term
        return value

    n_block, n_span = tokens // block, width // span

    def half_out(step):
        @pl.when(step % 2 == 0)
        def _():
            z_wait(step * 4)
            for r in range(n_block):
                hidden_block(step * 4, 0, r)

        @pl.loop(0, 4)
        def _(t):
            num = step * 4 + t
            k, b, i, g, s, p = order(num)
            piece_ahead(num)
            more = num % 8 < 7

            @pl.when(more)
            def _():
                z_wait(num + 1)
            ahead = jnp.where(more, num + 1, num)
            side = num % 2
            tile_open(k, s, p)
            for n in range(n_span):
                cols = slice(n * span, (n + 1) * span)
                value = product(lambda part: ht[side, :, part], lambda part, c: gin[part, c], cols)
                for r in range(n * n_block // n_span, (n + 1) * n_block // n_span):
                    hidden_block(ahead, 1 - side, r)
                emit_tile(k, s, p, cols, value)
            tile_close(k, s, p)

    def half_in(step):
        k, s = step // 2, step % 2
        b, i = k // 4, (k // 2) % 2
        j = 2 * i + jnp.where(s == 0, 1 - core, core)

        @pl.when(b == 0)
        def _():
            pltpu.make_async_copy(win2.at[:, pl.ds(pl.multiple_of(width * j, width), width)], winbuf, winsem).start()

        @pl.loop(0, 4)
        def _(p):
            num = step * 4 + p
            piece_ahead(num)
            z_wait(num)
            w_wait(num)
            slot = num % 3
            where = pl.ds(pl.multiple_of(p * tile, tile), tile)
            for r in range(n_block):
                part = slice(r * block, (r + 1) * block)
                back = dot_nt(gin[part, :], wbuf[slot])
                dz[part, where] = (back * gelu_slope(zbuf[slot, part, :].astype(F32))).astype(BF16)

        @pl.loop(0, 4)
        def _(p):
            lines = pl.ds(pl.multiple_of(p * tile, tile), tile)
            tile_open(k, s, p)
            for n in range(n_span):
                cols = slice(n * span, (n + 1) * span)
                emit_tile(k, s, p, cols, product(lambda part: xt[lines, part], lambda part, c: dz[part, c], cols))
            tile_close(k, s, p)

    def pass_back():
        pltpu.make_async_copy(win2.at[:, pl.ds(0, width)], winbuf, winsem).wait()

        @pl.loop(0, width // tile)
        def _(n):
            lines = pl.ds(pl.multiple_of(n * tile, tile), tile)
            for m in range(2):
                part = slice(m * micro, (m + 1) * micro)
                acc[part, lines] += dot_nt(dz[part, :], winbuf[lines, :])

    piece_start(0)
    first = pltpu.make_async_copy(dy, gin, gsem)
    first.start()
    piece_start(1)
    x_copy(x2).start()
    first.wait()
    pl.semaphore_wait(barrier, 6)

    @pl.loop(0, GRANULES + FIRST + 3 * LAG)
    def _(step):
        k, g, s = step // 2, (step // 2) % 2, step % 2

        @pl.when(step == 2)
        def _():
            @pl.loop(0, n_block)
            def _(r):
                part = pl.ds(pl.multiple_of(r * block, block), block)
                acc[part, :] = gin[part, :].astype(F32)

        @pl.when(step == N_CHUNK)
        def _():
            x_copy(x1).start()

            @pl.loop(0, n_block)
            def _(r):
                part = pl.ds(pl.multiple_of(r * block, block), block)
                gin[part, :] = acc[part, :].astype(BF16)

        @pl.when(jnp.logical_or(step == 2, step == N_CHUNK + 2))
        def _():
            x_copy(x2).wait()

            @pl.loop(0, n_block)
            def _(r):
                part = pl.ds(pl.multiple_of(r * block, block), block)
                for c in range(width // tile):
                    xt[c * tile:(c + 1) * tile, part] = dz[part, c * tile:(c + 1) * tile].T

        @pl.when(step < GRANULES)
        def _():
            @pl.when(g == 0)
            def _():
                half_out(step)

            @pl.when(g == 1)
            def _():
                half_in(step)

            @pl.when(jnp.logical_and(s == 1, k >= 1))
            def _():
                for h in range(2):
                    claim(A1, k >= 2)
                    claim(B1, k >= 2)
                    claim(C1, k >= 2)
                    for copy in phase1(2 * k + h):
                        copy.start()

            @pl.when(jnp.logical_and(g == 1, k < N_CHUNK // 2))
            def _():
                pass_back()
        service(step)

    for p in range(2):
        core_copy(p).wait_send()
    for q in range(2):
        fin_wait(GRANULES - 2 + q)
    for i in range(2):
        for h in range(2):
            for d in range(4):
                @pl.when(ix != d)
                def _():
                    remote(fin.at[0], fin.at[0], fin_send.at[0], fin_recv.at[i, h, d], to_core).wait_recv()


def scratch(dims):
    t, w, r, h, q = dims.tokens, dims.width, dims.rows, dims.half, dims.quarter
    a, b, c = dims.row_a, dims.row_b, dims.row_c
    tile = dims.tile
    V, DMA = pltpu.VMEM, pltpu.SemaphoreType.DMA
    return [
        V((t, w), BF16), V((w, t), BF16), V((t, w), F32), V((t, w), BF16), V((3, t, tile), BF16), V((3, tile, w), BF16), V((w, w), BF16),
        V((2, tile, t), BF16), V((2, tile, w), F32), V((4, tile, w), F32),
        V((2, 2, 2, 2, r, w), F32), V((4, 2, 2, 2, a, q), F32), V((4, 2, 2, b, h), F32), V((4, 2, 2, c, h), F32),
        V((2, 2, 2, 2, a, q), F32), V((2, 2, 2, b, h), F32), V((2, 2, 2, c, h), F32),
        V((4, 2, 2, a, q), F32), V((4, 2, 2, b, q), F32), V((4, 2, c, h), F32),
        V((2, 2, 2, a + b, q), F32), V((2, 2, c, h), F32), V((4, 2, a + b, q), F32), V((4, 2, c, q), F32),
        V((2, 2, a + b, q), F32), V((2, 2, c, q), F32), V((4, a + b, q), F32), V((4, c, q), F32), V((2, r, q), F32),
        DMA((3,)), DMA((3,)), DMA, DMA, DMA,
        DMA((2,)), DMA((4,)), DMA((4, 3)), DMA((4, 3)), DMA((4, 3)), DMA((4, 3)), DMA((4, 2)), DMA((4, 2)), DMA((4, 2)), DMA((4, 2)),
        DMA((2,)), DMA((2, 2, 4)), DMA((2,)), pltpu.SemaphoreType.REGULAR((11,)),
    ]


def solution(mesh):
    row_spec = P(('dz', 'dy', 'dx'), None)
    full_spec = P(None, None)

    def per_device(act_one, pre_one, act_two, pre_two, grad_out, w_in_two, w_out_one, w_out_two):
        dims = Dims(*grad_out.shape)
        any_spec = pl.BlockSpec(memory_space=pl.ANY)
        shard = pl.pallas_call(
            functools.partial(kernel, dims),
            out_shape=jax.ShapeDtypeStruct((4 * dims.rows, dims.width // 128, 128), F32),
            in_specs=[any_spec] * 8,
            out_specs=any_spec,
            scratch_shapes=scratch(dims),
            compiler_params=pltpu.CompilerParams(collective_id=0, has_side_effects=True, vmem_limit_bytes=67043328),
        )(pre_two, pre_one, act_two, act_one, grad_out, w_in_two, w_out_one, w_out_two)
        return shard.reshape(-1)

    return jax.shard_map(per_device, mesh=mesh, in_specs=(row_spec,) * 5 + (full_spec,) * 3, out_specs=P(('dx', 'dy', 'dz')), check_vma=False)
```

time: 340 us -> 305 us (0.90)
  Pallas kernels: 335 us -> 301 us
    pallas_call x1, Pallas kernels: 335 us -> 301 us  [per_device(): pl.pallas_call(functools.partial(kernel, dims), out_shape=jax.ShapeDtypeS...]
where the time goes in v2:
time: 305 us; the launch traced here: 304 us
  Pallas kernels  301 us (99%)
    pallas_call x1, Pallas kernels, per_device(): pl.pallas_call(functools.partial(kernel, dims), out_shape=jax.ShapeDtypeS...  301 us

profile of v2, /device:TPU:0, one launch (start us, length us, event | category | flops | bytes accessed | tf_op | source)
XLA Modules:
  0.0 304.4 jit_solution(5107842928246324914)
XLA Ops:
  0.0 301.3 %shard_map.82 = f32[512,8,128]{2,1,0:T(8,128)} custom-call(bf16[2048,4096]{1,0:T(8,128)(2,1)} %z2.1, bf16[2048,4096]{1,0:T(8,128)(2,1)} %z1.1, bf16[2048,1024]{1,0:T(8,128)(2,1)} %x2.1, bf16[2048,1024]{1,0:T(8,128)(2,1)} %x1.1, bf16[2048,1024]{1,0:T(8,128)(2,1)} %dy.1, bf16[1024,4096]{1,0:T(8,128)(2,1)} %win2.1, bf16[4096,1024]{1,0:T(8,128)(2,1)} %wo1.1, ...), custom_call_target="tpu_custom_call" | custom-call | tf_op jit(solution)/shard_map/pallas_call | solution.py:536
  301.3 3.0 %copy.10 = f32[524288]{0:T(1024)} copy(f32[524288]{0:T(1024)} %bitcast.1) | data formatting | bytes 4194304

commit v3 on v2

v3 whole, which is shorter than its diff:
```python
import functools

import jax
import jax.numpy as jnp
from jax import lax
from jax.experimental import pallas as pl
from jax.experimental.pallas import tpu as pltpu
from jax.sharding import PartitionSpec as P

MESH = pl.DeviceIdType.MESH
F32 = jnp.float32
BF16 = jnp.bfloat16
N_CHUNK = 8
GRANULES = 2 * N_CHUNK
TAKE = (
    (14, 16, 19, 20, 25, 28, 34, 41, 48, 49, 55, 56, 62, 64, 70, 72),
    (18, 20, 21, 23, 28, 30, 41, 49, 57, 58, 66, 67, 71, 74, 78, 79),
    (20, 23, 26, 30, 31, 38, 49, 57, 65, 69, 73, 77, 81, 84, 85, 88),
    (22, 27, 28, 32, 38, 48, 57, 68, 75, 76, 80, 82, 83, 86, 87, 89),
)
ROOT = 0.7978845608028654
CUBE = 0.044715


def gelu_hidden(pre):
    square = pre * pre
    bend = jnp.tanh(pre * (ROOT + (ROOT * CUBE) * square))
    half = 0.5 * pre
    return half + half * bend


def gelu_slope(pre):
    square = pre * pre
    bend = jnp.tanh(pre * (ROOT + (ROOT * CUBE) * square))
    tail = ((1.0 - bend * bend) * pre) * ((1.5 * ROOT * CUBE) * square + 0.5 * ROOT)
    return (0.5 + 0.5 * bend) + tail


def dot_nn(left, right):
    return lax.dot_general(left, right, (((1,), (0,)), ((), ())), preferred_element_type=F32)


def dot_nt(left, right):
    return lax.dot_general(left, right, (((1,), (1,)), ((), ())), preferred_element_type=F32)


class Dims:
    def __init__(self, tokens, width):
        self.tokens = tokens
        self.micro = tokens // 2
        self.width = width
        self.hidden = 4 * width
        self.rows = width // 8
        self.tile = 2 * self.rows
        self.half = width // 2
        self.quarter = width // 4
        unit = self.rows // 16
        self.row_a = max(8, (unit * 5) // 8 * 8)
        self.row_c = 4 * unit
        self.row_b = self.rows - self.row_a - self.row_c
        self.block = min(256, self.micro)
        self.span = min(512, width)


def kernel(dims, z2, z1, x2, x1, dy, win2, wo1, wo2, out,
           gin, xt, acc, dz, zbuf, wbuf, winbuf, ht, rcore,
           sums, r1a, r1b, r1c, s2a, s2b, s2c, r2a, r2b, r2c, s3ab, s3c, r3ab, r3c, s4ab, s4c, r4ab, r4c, fin,
           zsem, wsem, winsem, xsem, gsem,
           core_send, core_recv, send1, recv1, send2, recv2, send3, recv3, send4, recv4,
           fin_send, fin_recv, fin_local, credit):
    rows, tile, width, half, quarter = dims.rows, dims.tile, dims.width, dims.half, dims.quarter
    micro, tokens, block, span = dims.micro, dims.tokens, dims.block, dims.span
    row_a, row_b, row_c = dims.row_a, dims.row_b, dims.row_c
    row_ab = row_a + row_b
    lanes = 128
    iz, iy, ix = lax.axis_index('dz'), lax.axis_index('dy'), lax.axis_index('dx')
    px, core = ix // 2, ix % 2
    zhi, zlo = iz // 2, iz % 2
    to_core = (iz, iy, px * 2 + (1 - core))
    to_x = (iz, iy, (1 - px) * 2 + core)
    to_xc = (iz, iy, (1 - px) * 2 + (1 - core))
    to_y = (iz, 1 - iy, ix)
    to_za = (zhi * 2 + (1 - zlo), iy, ix)
    to_zb = ((1 - zhi) * 2 + zlo, iy, ix)
    keep_x = pl.ds(pl.multiple_of(px * quarter, min(quarter, lanes)), quarter)
    send_x = pl.ds(pl.multiple_of((1 - px) * quarter, min(quarter, lanes)), quarter)
    CORE, A1, B1, C1, A2, B2, C2, AB3, C3, AB4, C4 = range(11)

    barrier = pltpu.get_barrier_semaphore()
    for peer in (to_core, to_x, to_xc, to_y, to_za, to_zb):
        pl.semaphore_signal(barrier, inc=1, device_id=peer, device_id_type=MESH)

    def order(num):
        k, t = num // 8, num % 8
        b, g, i = k // 4, (k // 2) % 2, k % 2
        plain_s, plain_p = t // 4, t % 4
        first = jnp.logical_or(t == 0, jnp.logical_and(t % 2 == 1, t < 7))
        mixed_s = jnp.where(first, 0, 1)
        mixed_p = jnp.where(first, (t + 1) // 2, jnp.where(t == 7, 3, t // 2 - 1))
        s = jnp.where(g == 0, mixed_s, plain_s)
        p = jnp.where(g == 0, mixed_p, plain_p)
        return k, b, i, g, s, p

    def piece_start(num):
        k, b, i, g, s, p = order(num)
        j = 2 * i + jnp.where(s == 0, 1 - core, core)
        slot = num % 3

        def from_block(zref, wref, with_win):
            @pl.when(g == 0)
            def _():
                for h in range(2):
                    col = pl.multiple_of((dims.hidden // 8) * (2 * p + h) + rows * j, rows)
                    pltpu.make_async_copy(zref.at[:, pl.ds(col, rows)], zbuf.at[slot, :, pl.ds(h * rows, rows)], zsem.at[slot]).start()

            @pl.when(g == 1)
            def _():
                col = pl.multiple_of(width * j + tile * p, tile)
                pltpu.make_async_copy(zref.at[:, pl.ds(col, tile)], zbuf.at[slot], zsem.at[slot]).start()
                pltpu.make_async_copy(wref.at[pl.ds(col, tile), :], wbuf.at[slot], wsem.at[slot]).start()
                if with_win:
                    pltpu.make_async_copy(win2.at[:, pl.ds(col, tile)], winbuf.at[slot], winsem.at[slot]).start()

        @pl.when(b == 0)
        def _():
            from_block(z2, wo2, True)

        @pl.when(b == 1)
        def _():
            from_block(z1, wo1, False)

    def piece_ahead(num):
        @pl.when(num + 2 < 8 * N_CHUNK)
        def _():
            piece_start(num + 2)

    def z_wait(num):
        pltpu.make_async_copy(z2.at[:, pl.ds(0, tile)], zbuf.at[num % 3], zsem.at[num % 3]).wait()

    def w_wait(num):
        pltpu.make_async_copy(wo2.at[pl.ds(0, tile), :], wbuf.at[num % 3], wsem.at[num % 3]).wait()

    def win_wait(num):
        pltpu.make_async_copy(win2.at[:, pl.ds(0, tile)], winbuf.at[num % 3], winsem.at[num % 3]).wait()

    def x_copy(xref, c):
        return pltpu.make_async_copy(xref.at[:, pl.ds(c * tile, tile)], dz.at[c % 2], xsem.at[c % 2])

    def core_copy(p):
        return pltpu.make_async_remote_copy(sums.at[8 + p % 2], rcore.at[p], core_send.at[p % 2], core_recv.at[p], device_id=to_core, device_id_type=MESH)

    def remote(src, dst, sends, recvs, peer):
        return pltpu.make_async_remote_copy(src, dst, sends, recvs, device_id=peer, device_id_type=MESH)

    def shift(q, part, size):
        return pl.ds(pl.multiple_of((q % 2) * half + part, min(quarter, lanes)), size)

    def phase1(q):
        base, r = (q // 2) % 2 * 4, q % 4
        return (
            remote(sums.at[pl.ds(base, 4), :, pl.ds(0, row_a), shift(q, (1 - px) * quarter, quarter)], r1a.at[r], send1.at[r, 0], recv1.at[r, 0], to_x),
            remote(sums.at[pl.ds(base + 2 * (1 - iy), 2), :, pl.ds(row_a, row_b), shift(q, 0, half)], r1b.at[r], send1.at[r, 1], recv1.at[r, 1], to_y),
            remote(sums.at[pl.ds(base, 4), 1 - zlo, pl.ds(row_ab, row_c), shift(q, 0, half)], r1c.at[r], send1.at[r, 2], recv1.at[r, 2], to_za),
        )

    def phase1_early(q, p):
        base, r = (q // 2) % 2 * 4, q % 4
        remote(sums.at[base + p, :, pl.ds(0, row_a), shift(q, (1 - px) * quarter, quarter)], r1a.at[r, p], send1.at[r, 0], recv1.at[r, 0], to_x).start()
        remote(sums.at[base + p, 1 - zlo, pl.ds(row_ab, row_c), shift(q, 0, half)], r1c.at[r, p], send1.at[r, 2], recv1.at[r, 2], to_za).start()

        @pl.when(p // 2 != iy)
        def _():
            remote(sums.at[base + p, :, pl.ds(row_a, row_b), shift(q, 0, half)], r1b.at[r, p % 2], send1.at[r, 1], recv1.at[r, 1], to_y).start()

    def phase1_claim(q, now):
        for kind in (A1, B1, C1):
            claim(kind, jnp.logical_and(q >= 4, now))

    def phase2(q):
        r = v = q % 4
        return (
            remote(s2a.at[v, pl.ds(2 * (1 - iy), 2)], r2a.at[r], send2.at[r, 0], recv2.at[r, 0], to_y),
            remote(s2b.at[v, :, :, :, send_x], r2b.at[r], send2.at[r, 1], recv2.at[r, 1], to_x),
            remote(s2c.at[v, :, 1 - zhi], r2c.at[r], send2.at[r, 2], recv2.at[r, 2], to_zb),
        )

    def phase3(q):
        r = v = q % 4
        return (
            remote(s3ab.at[v, :, 1 - zlo], r3ab.at[r], send3.at[r, 0], recv3.at[r, 0], to_za),
            remote(s3c.at[v, :, :, send_x], r3c.at[r], send3.at[r, 1], recv3.at[r, 1], to_x),
        )

    def phase4(q):
        r = v = q % 4
        return (
            remote(s4ab.at[v, 1 - zhi], r4ab.at[r], send4.at[r, 0], recv4.at[r, 0], to_zb),
            remote(s4c.at[v, 1 - iy], r4c.at[r], send4.at[r, 1], recv4.at[r, 1], to_y),
        )

    def grant(kind, peer, ok):
        @pl.when(ok)
        def _():
            pl.semaphore_signal(credit.at[kind], inc=1, device_id=peer, device_id_type=MESH)

    def claim(kind, ok):
        @pl.when(ok)
        def _():
            pl.semaphore_wait(credit.at[kind], 1)

    def out_place(q, n):
        i, h = (q // 2) % 2, q % 2
        j = 2 * i + core
        strip = (width // lanes // 2) * h + (width // lanes // 4) * px + n
        return (
            out.at[pl.ds(pl.multiple_of(j * rows, rows), rows), strip, :],
            out.reshape(rows, 4, width // lanes, lanes).at[:, j, strip, :],
        )

    def owner_of(q):
        return q // 4

    def fin_start(q):
        f = q % 2
        for g in range(2):
            @pl.when((q // 4) % 2 == g)
            def _():
                for n in range(quarter // lanes):
                    strip = fin.at[f, :, pl.ds(n * lanes, lanes)]
                    place = out_place(q, n)[g]

                    @pl.when(owner_of(q) == ix)
                    def _():
                        pltpu.make_async_copy(strip, place, fin_local.at[f]).start()

                    @pl.when(owner_of(q) != ix)
                    def _():
                        remote(strip, place, fin_send.at[f], fin_recv.at[(q // 2) % 2, q % 2, ix], (iz, iy, owner_of(q))).start()

    def fin_wait(q):
        f = q % 2

        @pl.when(owner_of(q) == ix)
        def _():
            pltpu.make_async_copy(fin.at[f], fin.at[f], fin_local.at[f]).wait()

        @pl.when(owner_of(q) != ix)
        def _():
            remote(fin.at[f], fin.at[f], fin_send.at[f], fin_recv.at[0, 0, ix], to_core).wait_send()

    def service(num):
        def stage_of(phase, act):
            q, through = 0, 0
            for when in TAKE[phase - 1]:
                q = q + jnp.where(num > when, 1, 0)
                through = through + jnp.where(num >= when, 1, 0)

            @pl.when(through > q)
            def _():
                act(q, q % 4, q % 4, q < GRANULES - 4, q >= 4)

        def take4(q, r, v, more, later):
            ab, c = phase4(q)

            @pl.when(q >= 2)
            def _():
                fin_wait(q - 2)
            ab.wait()
            f = q % 2
            fin[f, 0:row_ab, :] = s4ab[v, zhi] + r4ab[r]
            grant(AB4, to_zb, more)
            c.wait()
            fin[f, row_ab:rows, :] = s4c[v, iy] + r4c[r]
            grant(C4, to_y, more)
            fin_start(q)

        def take3(q, r, v, more, later):
            ab, c = phase3(q)
            ab4, c4 = phase4(q)
            ab.wait()
            s4ab[v] = s3ab[v, :, zlo] + r3ab[r]
            grant(AB3, to_za, more)
            claim(AB4, later)
            ab4.start()
            c.wait()
            s4c[v] = s3c[v, :, :, keep_x] + r3c[r]
            grant(C3, to_x, more)
            claim(C4, later)
            c4.start()

        def take2(q, r, v, more, later):
            a, b, c = phase2(q)
            ab3, c3 = phase3(q)
            a.wait()
            s3ab[v, :, :, 0:row_a, :] = s2a[v, pl.ds(2 * iy, 2)] + r2a[r]
            grant(A2, to_y, more)
            b.wait()
            s3ab[v, :, :, row_a:row_ab, :] = s2b[v, :, :, :, keep_x] + r2b[r]
            grant(B2, to_x, more)
            claim(AB3, later)
            ab3.start()
            c.wait()
            s3c[v] = s2c[v, :, zhi] + r2c[r]
            grant(C2, to_zb, more)
            claim(C3, later)
            c3.start()

        def take1(q, r, v, more, later):
            base = (q // 2) % 2 * 4
            a, b, c = phase1(q)
            a2, b2, c2 = phase2(q)
            a.wait()
            s2a[v] = sums[pl.ds(base, 4), :, 0:row_a, shift(q, px * quarter, quarter)] + r1a[r]
            grant(A1, to_x, more)
            claim(A2, later)
            a2.start()
            b.wait()
            s2b[v] = sums[pl.ds(base + 2 * iy, 2), :, row_a:row_ab, shift(q, 0, half)] + r1b[r]
            grant(B1, to_y, more)
            claim(B2, later)
            b2.start()
            c.wait()
            s2c[v] = (sums[pl.ds(base, 4), zlo, row_ab:rows, shift(q, 0, half)] + r1c[r]).reshape(2, 2, row_c, half)
            grant(C1, to_za, more)
            claim(C2, later)
            c2.start()

        stage_of(4, take4)
        stage_of(3, take3)
        stage_of(2, take2)
        stage_of(1, take1)

    def emit(to, into, source, cols, value):
        for h in range(2):
            sums[to, h, :, into] = value[h * rows:(h + 1) * rows] + rcore[source, h, :, cols]

    def tile_open(k, s, p):
        @pl.when(s == 0)
        def _():
            @pl.when(jnp.logical_or(k >= 1, p >= 2))
            def _():
                core_copy(p).wait_send()

        @pl.when(s == 1)
        def _():
            core_copy(p).wait_recv()

    def tile_close(k, s, p):
        @pl.when(s == 0)
        def _():
            claim(CORE, k >= 1)
            core_copy(p).start()

        @pl.when(s == 1)
        def _():
            grant(CORE, to_core, k < N_CHUNK - 1)

    def hidden_block(num, side, r):
        part = slice(r * block, (r + 1) * block)
        ht[side, :, part] = gelu_hidden(zbuf[num % 3, part, :].astype(F32)).astype(BF16).T

    def slope_block(num, side, r):
        part = slice(r * block, (r + 1) * block)
        back = dot_nt(gin[part, :], wbuf[num % 3])
        dz[side, part, :] = (back * gelu_slope(zbuf[num % 3, part, :].astype(F32))).astype(BF16)

    def rounded(value):
        return value.astype(BF16).astype(F32)

    n_block, n_span = tokens // block, width // span
    micros = [slice(m * micro, (m + 1) * micro) for m in range(2)]

    def tile_out(num):
        k, b, i, g, s, p = order(num)

        @pl.when(num % 32 == 0)
        def _():
            z_wait(num)
            for r in range(n_block):
                hidden_block(num, 0, r)

        @pl.when(num == 0)
        def _():
            first.wait()
            pl.semaphore_wait(barrier, 6)
        piece_ahead(num)
        more = num % 16 < 15

        @pl.when(more)
        def _():
            z_wait(num + 1)
        ahead = jnp.where(more, num + 1, num)
        side = num % 2
        tile_open(k, s, p)
        to = jnp.where(s == 0, 8 + p % 2, k % 2 * 4 + p)
        source = jnp.where(s == 0, 4, p)
        for n in range(n_span):
            cols = slice(n * span, (n + 1) * span)
            value = rounded(dot_nn(ht[side, :, micros[0]], gin[micros[0], cols])) + rounded(dot_nn(ht[side, :, micros[1]], gin[micros[1], cols]))
            for r in range(n * n_block // n_span, (n + 1) * n_block // n_span):
                hidden_block(ahead, 1 - side, r)
            emit(to, cols, source, cols, value)
        tile_close(k, s, p)

        @pl.when(s == 1)
        def _():
            for h in range(2):
                phase1_claim(2 * k + h, p == 0)
                phase1_early(2 * k + h, p)

    def tile_in(num):
        k, b, i, g, s, p = order(num)

        @pl.when(num % 32 == 16)
        def _():
            z_wait(num)
            w_wait(num)
            for r in range(n_block):
                slope_block(num, 0, r)
        piece_ahead(num)
        more = num % 16 < 15

        @pl.when(more)
        def _():
            z_wait(num + 1)
            w_wait(num + 1)
        ahead = jnp.where(more, num + 1, num)
        side = num % 2
        tile_open(k, s, p)
        source = jnp.where(s == 0, 4, p)
        for r in range(4):
            lines = slice(r * tile, (r + 1) * tile)
            to = jnp.where(s == 0, 8 + p % 2, k % 2 * 4 + r)
            into = pl.ds(pl.multiple_of(jnp.where(s == 0, r, p) * tile, tile), tile)
            spread = [range(r * n_block // 4 + m * n_block // 8, r * n_block // 4 + (m + 1) * n_block // 8) for m in range(2)]
            value = rounded(dot_nn(xt[lines, micros[0]], dz[side, micros[0], :]))
            for e in spread[0]:
                slope_block(ahead, 1 - side, e)
            value = value + rounded(dot_nn(xt[lines, micros[1]], dz[side, micros[1], :]))
            for e in spread[1]:
                slope_block(ahead, 1 - side, e)
            emit(to, into, source, lines, value)
        tile_close(k, s, p)

        @pl.when(jnp.logical_and(s == 1, p % 2 == 1))
        def _():
            q = 2 * k + p // 2
            phase1_claim(q, True)
            for copy in phase1(q):
                copy.start()

        @pl.when(b == 0)
        def _():
            win_wait(num)
            for r in range(n_block):
                part = slice(r * block, (r + 1) * block)
                acc[part, :] += dot_nt(dz[side, part, :], winbuf[num % 3])

    piece_start(0)
    first = pltpu.make_async_copy(dy, gin, gsem)
    first.start()
    piece_start(1)
    for c in range(2):
        x_copy(x2, c).start()
    rcore[4] = jnp.zeros((2, rows, width), F32)

    def turn(xref):
        for c in range(4):
            x_copy(xref, c).wait()

            @pl.loop(0, n_block)
            def _(r):
                part = pl.ds(pl.multiple_of(r * block, block), block)
                xt[c * tile:(c + 1) * tile, part] = dz[c % 2, part, :].T
            if c < 2:
                x_copy(xref, c + 2).start()

    tiles = 8 * N_CHUNK

    @pl.loop(0, max(max(row) for row in TAKE) + 1)
    def _(num):
        @pl.when(num == tiles // 4)
        def _():
            @pl.loop(0, n_block)
            def _(r):
                part = pl.ds(pl.multiple_of(r * block, block), block)
                acc[part, :] = gin[part, :].astype(F32)
            turn(x2)

        @pl.when(num == tiles // 2)
        def _():
            for c in range(2):
                x_copy(x1, c).start()

            @pl.loop(0, n_block)
            def _(r):
                part = pl.ds(pl.multiple_of(r * block, block), block)
                gin[part, :] = acc[part, :].astype(BF16)

        @pl.when(num == 3 * tiles // 4)
        def _():
            turn(x1)

        @pl.when(jnp.logical_and(num < tiles, num % 32 < 16))
        def _():
            tile_out(num)

        @pl.when(jnp.logical_and(num < tiles, num % 32 >= 16))
        def _():
            tile_in(num)
        service(num)

    for p in range(2):
        core_copy(p).wait_send()
    for q in range(2):
        fin_wait(GRANULES - 2 + q)
    for i in range(2):
        for h in range(2):
            for d in range(4):
                @pl.when(ix != d)
                def _():
                    remote(fin.at[0], fin.at[0], fin_send.at[0], fin_recv.at[i, h, d], to_core).wait_recv()


def scratch(dims):
    t, w, r, h, q = dims.tokens, dims.width, dims.rows, dims.half, dims.quarter
    a, b, c = dims.row_a, dims.row_b, dims.row_c
    tile = dims.tile
    V, DMA = pltpu.VMEM, pltpu.SemaphoreType.DMA
    return [
        V((t, w), BF16), V((w, t), BF16), V((t, w), F32), V((2, t, tile), BF16), V((3, t, tile), BF16), V((3, tile, w), BF16), V((3, w, tile), BF16),
        V((2, tile, t), BF16), V((5, 2, r, w), F32),
        V((10, 2, r, w), F32), V((4, 4, 2, a, q), F32), V((4, 2, 2, b, h), F32), V((4, 4, c, h), F32),
        V((4, 4, 2, a, q), F32), V((4, 2, 2, b, h), F32), V((4, 2, 2, c, h), F32),
        V((4, 2, 2, a, q), F32), V((4, 2, 2, b, q), F32), V((4, 2, c, h), F32),
        V((4, 2, 2, a + b, q), F32), V((4, 2, c, h), F32), V((4, 2, a + b, q), F32), V((4, 2, c, q), F32),
        V((4, 2, a + b, q), F32), V((4, 2, c, q), F32), V((4, a + b, q), F32), V((4, c, q), F32), V((2, r, q), F32),
        DMA((3,)), DMA((3,)), DMA((3,)), DMA((2,)), DMA,
        DMA((2,)), DMA((4,)), DMA((4, 3)), DMA((4, 3)), DMA((4, 3)), DMA((4, 3)), DMA((4, 2)), DMA((4, 2)), DMA((4, 2)), DMA((4, 2)),
        DMA((2,)), DMA((2, 2, 4)), DMA((2,)), pltpu.SemaphoreType.REGULAR((11,)),
    ]


def solution(mesh):
    row_spec = P(('dz', 'dy', 'dx'), None)
    full_spec = P(None, None)

    def per_device(act_one, pre_one, act_two, pre_two, grad_out, w_in_two, w_out_one, w_out_two):
        dims = Dims(*grad_out.shape)
        any_spec = pl.BlockSpec(memory_space=pl.ANY)
        shard = pl.pallas_call(
            functools.partial(kernel, dims),
            out_shape=jax.ShapeDtypeStruct((4 * dims.rows, dims.width // 128, 128), F32),
            in_specs=[any_spec] * 8,
            out_specs=any_spec,
            scratch_shapes=scratch(dims),
            compiler_params=pltpu.CompilerParams(collective_id=0, has_side_effects=True, vmem_limit_bytes=67043328),
        )(pre_two, pre_one, act_two, act_one, grad_out, w_in_two, w_out_one, w_out_two)
        return shard.reshape(-1)

    return jax.shard_map(per_device, mesh=mesh, in_specs=(row_spec,) * 5 + (full_spec,) * 3, out_specs=P(('dx', 'dy', 'dz')), check_vma=False)
```

time: 305 us -> 288 us (0.944)
  Pallas kernels: 301 us -> 285 us
    pallas_call x1, Pallas kernels: 301 us -> 285 us  [per_device(): pl.pallas_call(functools.partial(kernel, dims), out_shape=jax.ShapeDtypeS...]
where the time goes in v3:
time: 288 us
  Pallas kernels  285 us (99%)
  local copies, waits for them, and re-layouts  3.05 us (1%)
    pallas_call x1, Pallas kernels, per_device(): pl.pallas_call(functools.partial(kernel, dims), out_shape=jax.ShapeDtypeS...  285 us

profile of v3, /device:TPU:0, one launch (start us, length us, event | category | flops | bytes accessed | tf_op | source)
XLA Modules:
  0.0 287.7 jit_solution(13000066524551420196)
XLA Ops:
  0.0 284.6 %shard_map.82 = f32[512,8,128]{2,1,0:T(8,128)} custom-call(bf16[2048,4096]{1,0:T(8,128)(2,1)} %z2.1, bf16[2048,4096]{1,0:T(8,128)(2,1)} %z1.1, bf16[2048,1024]{1,0:T(8,128)(2,1)} %x2.1, bf16[2048,1024]{1,0:T(8,128)(2,1)} %x1.1, bf16[2048,1024]{1,0:T(8,128)(2,1)} %dy.1, bf16[1024,4096]{1,0:T(8,128)(2,1)} %win2.1, bf16[4096,1024]{1,0:T(8,128)(2,1)} %wo1.1, ...), custom_call_target="tpu_custom_call" | custom-call | tf_op jit(solution)/shard_map/pallas_call | solution.py:551
  284.6 3.0 %copy.10 = f32[524288]{0:T(1024)} copy(f32[524288]{0:T(1024)} %bitcast.1) | data formatting | bytes 4194304

commit v4 on v3

--- a/solution.py
+++ b/solution.py
@@ -12,12 +12,14 @@
 BF16 = jnp.bfloat16
 N_CHUNK = 8
 GRANULES = 2 * N_CHUNK
+FIN_SLOTS = 8
 TAKE = (
-    (14, 16, 19, 20, 25, 28, 34, 41, 48, 49, 55, 56, 62, 64, 70, 72),
-    (18, 20, 21, 23, 28, 30, 41, 49, 57, 58, 66, 67, 71, 74, 78, 79),
-    (20, 23, 26, 30, 31, 38, 49, 57, 65, 69, 73, 77, 81, 84, 85, 88),
-    (22, 27, 28, 32, 38, 48, 57, 68, 75, 76, 80, 82, 83, 86, 87, 89),
+    (14, 16, 19, 21, 24, 27, 32, 41, 48, 49, 54, 58, 60, 68, 69, 70),
+    (18, 20, 23, 26, 27, 30, 48, 49, 56, 59, 64, 69, 71, 72, 77, 80),
+    (22, 27, 31, 37, 47, 50, 59, 65, 67, 70, 74, 76, 79, 81, 83, 85),
+    (26, 40, 48, 61, 63, 66, 73, 75, 78, 79, 81, 82, 84, 86, 87, 88),
 )
+STEPS = TAKE + (tuple(TAKE[3][-1] + when for when in (-1, 0, 1, 2)),)
 ROOT = 0.7978845608028654
 CUBE = 0.044715
 
@@ -64,7 +66,7 @@
 
 def kernel(dims, z2, z1, x2, x1, dy, win2, wo1, wo2, out,
            gin, xt, acc, dz, zbuf, wbuf, winbuf, ht, rcore,
-           sums, r1a, r1b, r1c, s2a, s2b, s2c, r2a, r2b, r2c, s3ab, s3c, r3ab, r3c, s4ab, s4c, r4ab, r4c, fin,
+           sums, r1a, r1b, r1c, s2a, s2b, s2c, r2a, r2b, r2c, s3ab, s3c, r3ab, r3c, s4ab, s4c, r4ab, r4c, fin, shard,
            zsem, wsem, winsem, xsem, gsem,
            core_send, core_recv, send1, recv1, send2, recv2, send3, recv3, send4, recv4,
            fin_send, fin_recv, fin_local, credit):
@@ -208,50 +210,55 @@
         def _():
             pl.semaphore_wait(credit.at[kind], 1)
 
-    def out_place(q, n):
+    def shard_place(q):
         i, h = (q // 2) % 2, q % 2
-        j = 2 * i + core
-        strip = (width // lanes // 2) * h + (width // lanes // 4) * px + n
-        return (
-            out.at[pl.ds(pl.multiple_of(j * rows, rows), rows), strip, :],
-            out.reshape(rows, 4, width // lanes, lanes).at[:, j, strip, :],
-        )
+        return 2 * i + core, pl.ds(pl.multiple_of(half * h + quarter * px, lanes), quarter)
 
     def owner_of(q):
         return q // 4
 
     def fin_start(q):
-        f = q % 2
+        f = q % FIN_SLOTS
+        j, cols = shard_place(q)
+
+        @pl.when(owner_of(q) == ix)
+        def _():
+            shard[j, :, cols] = fin[f]
+
+        @pl.when(owner_of(q) != ix)
+        def _():
+            remote(fin.at[f], shard.at[j, :, cols], fin_send.at[f], fin_recv.at[(q // 2) % 2, q % 2, ix], (iz, iy, owner_of(q))).start()
+
+    def fin_wait(q):
+        f = q % FIN_SLOTS
+
+        @pl.when(owner_of(q) != ix)
+        def _():
+            remote(fin.at[f], fin.at[f], fin_send.at[f], fin_recv.at[0, 0, ix], to_core).wait_send()
+
+    def part_out(q):
+        i, h = (q // 2) % 2, q % 2
+        for d in range(4):
+            @pl.when(ix != d)
+            def _():
+                remote(fin.at[0], fin.at[0], fin_send.at[0], fin_recv.at[i, h, d], to_core).wait_recv()
         for g in range(2):
-            @pl.when((q // 4) % 2 == g)
-            def _():
-                for n in range(quarter // lanes):
-                    strip = fin.at[f, :, pl.ds(n * lanes, lanes)]
-                    place = out_place(q, n)[g]
-
-                    @pl.when(owner_of(q) == ix)
-                    def _():
-                        pltpu.make_async_copy(strip, place, fin_local.at[f]).start()
-
-                    @pl.when(owner_of(q) != ix)
-                    def _():
-                        remote(strip, place, fin_send.at[f], fin_recv.at[(q // 2) % 2, q % 2, ix], (iz, iy, owner_of(q))).start()
-
-    def fin_wait(q):
-        f = q % 2
-
-        @pl.when(owner_of(q) == ix)
-        def _():
-            pltpu.make_async_copy(fin.at[f], fin.at[f], fin_local.at[f]).wait()
-
-        @pl.when(owner_of(q) != ix)
-        def _():
-            remote(fin.at[f], fin.at[f], fin_send.at[f], fin_recv.at[0, 0, ix], to_core).wait_send()
+            @pl.when(core == g)
+            def _():
+                for c in range(2):
+                    j = 2 * i + c
+                    for n in range(half // lanes):
+                        strip = (half // lanes) * h + n
+                        if g == 0:
+                            place = out.at[pl.ds(pl.multiple_of(j * rows, rows), rows), strip, :]
+                        else:
+                            place = out.reshape(rows, 4, width // lanes, lanes).at[:, j, strip, :]
+                        pltpu.make_async_copy(shard.at[j, :, pl.ds(pl.multiple_of(strip * lanes, lanes), lanes)], place, fin_local).start()
 
     def service(num):
         def stage_of(phase, act):
             q, through = 0, 0
-            for when in TAKE[phase - 1]:
+            for when in STEPS[phase - 1]:
                 q = q + jnp.where(num > when, 1, 0)
                 through = through + jnp.where(num >= when, 1, 0)
 
@@ -262,11 +269,11 @@
         def take4(q, r, v, more, later):
             ab, c = phase4(q)
 
-            @pl.when(q >= 2)
-            def _():
-                fin_wait(q - 2)
+            @pl.when(q >= FIN_SLOTS)
+            def _():
+                fin_wait(q - FIN_SLOTS)
             ab.wait()
-            f = q % 2
+            f = q % FIN_SLOTS
             fin[f, 0:row_ab, :] = s4ab[v, zhi] + r4ab[r]
             grant(AB4, to_zb, more)
             c.wait()
@@ -330,6 +337,10 @@
         stage_of(2, take2)
         stage_of(1, take1)
 
+        def part(q, r, v, more, later):
+            part_out(q)
+        stage_of(5, part)
+
     def emit(to, into, source, cols, value):
         for h in range(2):
             sums[to, h, :, into] = value[h * rows:(h + 1) * rows] + rcore[source, h, :, cols]
@@ -477,7 +488,7 @@
 
     tiles = 8 * N_CHUNK
 
-    @pl.loop(0, max(max(row) for row in TAKE) + 1)
+    @pl.loop(0, max(max(row) for row in STEPS) + 1)
     def _(num):
         @pl.when(num == tiles // 4)
         def _():
@@ -512,14 +523,9 @@
 
     for p in range(2):
         core_copy(p).wait_send()
-    for q in range(2):
-        fin_wait(GRANULES - 2 + q)
-    for i in range(2):
-        for h in range(2):
-            for d in range(4):
-                @pl.when(ix != d)
-                def _():
-                    remote(fin.at[0], fin.at[0], fin_send.at[0], fin_recv.at[i, h, d], to_core).wait_recv()
+    pltpu.make_async_copy(out.at[pl.ds(0, 4 * rows)], out.at[pl.ds(0, 4 * rows)], fin_local).wait()
+    for q in range(FIN_SLOTS):
+        fin_wait(GRANULES - FIN_SLOTS + q)
 
 
 def scratch(dims):
@@ -534,10 +540,10 @@
         V((4, 4, 2, a, q), F32), V((4, 2, 2, b, h), F32), V((4, 2, 2, c, h), F32),
         V((4, 2, 2, a, q), F32), V((4, 2, 2, b, q), F32), V((4, 2, c, h), F32),
         V((4, 2, 2, a + b, q), F32), V((4, 2, c, h), F32), V((4, 2, a + b, q), F32), V((4, 2, c, q), F32),
-        V((4, 2, a + b, q), F32), V((4, 2, c, q), F32), V((4, a + b, q), F32), V((4, c, q), F32), V((2, r, q), F32),
+        V((4, 2, a + b, q), F32), V((4, 2, c, q), F32), V((4, a + b, q), F32), V((4, c, q), F32), V((FIN_SLOTS, r, q), F32), V((4, r, w), F32),
         DMA((3,)), DMA((3,)), DMA((3,)), DMA((2,)), DMA,
         DMA((2,)), DMA((4,)), DMA((4, 3)), DMA((4, 3)), DMA((4, 3)), DMA((4, 3)), DMA((4, 2)), DMA((4, 2)), DMA((4, 2)), DMA((4, 2)),
-        DMA((2,)), DMA((2, 2, 4)), DMA((2,)), pltpu.SemaphoreType.REGULAR((11,)),
+        DMA((FIN_SLOTS,)), DMA((2, 2, 4)), DMA, pltpu.SemaphoreType.REGULAR((11,)),
     ]
 
 

time: 288 us -> 281 us (0.976)
  Pallas kernels: 285 us -> 277 us
    pallas_call x1, Pallas kernels: 285 us -> 277 us  [per_device(): pl.pallas_call(functools.partial(kernel, dims), out_shape=jax.ShapeDtypeS...]
where the time goes in v4:
time: 281 us; the launch traced here: 280 us
  Pallas kernels  277 us (99%)
  local copies, waits for them, and re-layouts  3.05 us (1%)
    pallas_call x1, Pallas kernels, per_device(): pl.pallas_call(functools.partial(kernel, dims), out_shape=jax.ShapeDtypeS...  277 us

profile of v4, /device:TPU:0, one launch (start us, length us, event | category | flops | bytes accessed | tf_op | source)
XLA Modules:
  0.0 280.0 jit_solution(8802126487990584241)
XLA Ops:
  0.0 276.9 %shard_map.82 = f32[512,8,128]{2,1,0:T(8,128)} custom-call(bf16[2048,4096]{1,0:T(8,128)(2,1)} %z2.1, bf16[2048,4096]{1,0:T(8,128)(2,1)} %z1.1, bf16[2048,1024]{1,0:T(8,128)(2,1)} %x2.1, bf16[2048,1024]{1,0:T(8,128)(2,1)} %x1.1, bf16[2048,1024]{1,0:T(8,128)(2,1)} %dy.1, bf16[1024,4096]{1,0:T(8,128)(2,1)} %win2.1, bf16[4096,1024]{1,0:T(8,128)(2,1)} %wo1.1, ...), custom_call_target="tpu_custom_call" | custom-call | tf_op jit(solution)/shard_map/pallas_call | solution.py:557
  277.0 3.0 %copy.10 = f32[524288]{0:T(1024)} copy(f32[524288]{0:T(1024)} %bitcast.1) | data formatting | bytes 4194304

commit v5 on v4

--- a/solution.py
+++ b/solution.py
@@ -14,10 +14,10 @@
 GRANULES = 2 * N_CHUNK
 FIN_SLOTS = 8
 TAKE = (
-    (14, 16, 19, 21, 24, 27, 32, 41, 48, 49, 54, 58, 60, 68, 69, 70),
-    (18, 20, 23, 26, 27, 30, 48, 49, 56, 59, 64, 69, 71, 72, 77, 80),
-    (22, 27, 31, 37, 47, 50, 59, 65, 67, 70, 74, 76, 79, 81, 83, 85),
-    (26, 40, 48, 61, 63, 66, 73, 75, 78, 79, 81, 82, 84, 86, 87, 88),
+    (14, 15, 18, 20, 24, 26, 33, 38, 48, 50, 54, 59, 61, 64, 69, 71),
+    (18, 20, 25, 26, 27, 28, 48, 50, 56, 59, 65, 68, 71, 72, 75, 76),
+    (20, 23, 27, 32, 41, 43, 52, 57, 66, 70, 74, 75, 78, 80, 82, 85),
+    (24, 29, 40, 52, 56, 67, 73, 74, 76, 77, 79, 81, 83, 84, 86, 87),
 )
 STEPS = TAKE + (tuple(TAKE[3][-1] + when for when in (-1, 0, 1, 2)),)
 ROOT = 0.7978845608028654
@@ -257,13 +257,15 @@
 
     def service(num):
         def stage_of(phase, act):
-            q, through = 0, 0
-            for when in STEPS[phase - 1]:
-                q = q + jnp.where(num > when, 1, 0)
-                through = through + jnp.where(num >= when, 1, 0)
-
-            @pl.when(through > q)
-            def _():
+            due = num == STEPS[phase - 1][0]
+            for when in STEPS[phase - 1][1:]:
+                due = jnp.logical_or(due, num == when)
+
+            @pl.when(due)
+            def _():
+                q = 0
+                for when in STEPS[phase - 1]:
+                    q = q + jnp.where(num > when, 1, 0)
                 act(q, q % 4, q % 4, q < GRANULES - 4, q >= 4)
 
         def take4(q, r, v, more, later):
@@ -463,16 +465,23 @@
         @pl.when(b == 0)
         def _():
             win_wait(num)
-            for r in range(n_block):
-                part = slice(r * block, (r + 1) * block)
-                acc[part, :] += dot_nt(dz[side, part, :], winbuf[num % 3])
+
+            @pl.when(num == 16)
+            def _():
+                for r in range(n_block):
+                    part = slice(r * block, (r + 1) * block)
+                    acc[part, :] = gin[part, :].astype(F32) + dot_nt(dz[side, part, :], winbuf[num % 3])
+
+            @pl.when(num != 16)
+            def _():
+                for r in range(n_block):
+                    part = slice(r * block, (r + 1) * block)
+                    acc[part, :] += dot_nt(dz[side, part, :], winbuf[num % 3])
 
     piece_start(0)
     first = pltpu.make_async_copy(dy, gin, gsem)
     first.start()
     piece_start(1)
-    for c in range(2):
-        x_copy(x2, c).start()
     rcore[4] = jnp.zeros((2, rows, width), F32)
 
     def turn(xref):
@@ -490,12 +499,13 @@
 
     @pl.loop(0, max(max(row) for row in STEPS) + 1)
     def _(num):
+        @pl.when(num == N_CHUNK)
+        def _():
+            for c in range(2):
+                x_copy(x2, c).start()
+
         @pl.when(num == tiles // 4)
         def _():
-            @pl.loop(0, n_block)
-            def _(r):
-                part = pl.ds(pl.multiple_of(r * block, block), block)
-                acc[part, :] = gin[part, :].astype(F32)
             turn(x2)
 
         @pl.when(num == tiles // 2)

time: 281 us -> 280 us (level)
  no operation moved by 1% of the time
where the time goes in v5:
time: 280 us; the launch traced here: 279 us
  Pallas kernels  276 us (99%)
  local copies, waits for them, and re-layouts  3.05 us (1%)
    pallas_call x1, Pallas kernels, per_device(): pl.pallas_call(functools.partial(kernel, dims), out_shape=jax.ShapeDtypeS...  276 us

profile of v5, /device:TPU:0, one launch (start us, length us, event | category | flops | bytes accessed | tf_op | source)
XLA Modules:
  0.0 279.2 jit_solution(17496149194862514637)
XLA Ops:
  0.0 276.2 %shard_map.82 = f32[512,8,128]{2,1,0:T(8,128)} custom-call(bf16[2048,4096]{1,0:T(8,128)(2,1)} %z2.1, bf16[2048,4096]{1,0:T(8,128)(2,1)} %z1.1, bf16[2048,1024]{1,0:T(8,128)(2,1)} %x2.1, bf16[2048,1024]{1,0:T(8,128)(2,1)} %x1.1, bf16[2048,1024]{1,0:T(8,128)(2,1)} %dy.1, bf16[1024,4096]{1,0:T(8,128)(2,1)} %win2.1, bf16[4096,1024]{1,0:T(8,128)(2,1)} %wo1.1, ...), custom_call_target="tpu_custom_call" | custom-call | tf_op jit(solution)/shard_map/pallas_call | solution.py:567
  276.2 3.0 %copy.10 = f32[524288]{0:T(1024)} copy(f32[524288]{0:T(1024)} %bitcast.1) | data formatting | bytes 4194304
